TPU v7x, 32 devices: a whole 2x2x4 slice. The times are simulated.
32 devices in a mesh: seq: 8 (over y, x, core), stretch: 4 (over z).
Axes of the slice: x: 2, y: 2, z: 4, core: 2. Of those that a mesh axis runs over, the one named last changes fastest.
Arguments:
- queries: bfloat16 [4096, 1792], P(('stretch', 'seq')), may hold values from -140 to 140
- keys: bfloat16 [4096, 256], P(('stretch', 'seq')), may hold values from -6 to 6
- values: bfloat16 [4096, 256], P(('stretch', 'seq')), may hold values from -6 to 6
Outputs:
- attended: bfloat16 [4096, 1792], P(('stretch', 'seq'))
All inputs are finite; a program needn't handle non-finite values.
Results may differ from a plain program's by a relative error of at most 0.011.
Values may be sent and summed in bfloat16 or wider, within the bound.
A program may use at most 64 MiB of HBM per device.

v0:
```python
import functools
import math

import jax
import jax.numpy as jnp
import numpy as np
from jax import lax
from jax.experimental import pallas as pl
from jax.experimental.pallas import tpu as pltpu
from jax.sharding import PartitionSpec as P

QUERY_HEADS = 14
KEY_VALUE_HEADS = 2
HEAD_SIZE = 128
BLOCKS = 4
CLUSTER = QUERY_HEADS // KEY_VALUE_HEADS
WIDTH = CLUSTER * HEAD_SIZE
UNROLL = CLUSTER
SCALE = math.log2(math.e) / math.sqrt(HEAD_SIZE)


def rotary_table(positions):
    half = HEAD_SIZE // 2
    inverse = 10000000.0 ** (-(np.arange(half, dtype=np.float64) * 2.0) / HEAD_SIZE)
    angles = np.arange(positions, dtype=np.float64)[:, None] * inverse[None, :]
    return np.concatenate([np.cos(angles), np.sin(angles)], axis=1).astype(np.float32)


def factors(table):
    swapped = pltpu.roll(table, HEAD_SIZE // 2, 1)
    low = lax.broadcasted_iota(jnp.int32, table.shape, 1) < HEAD_SIZE // 2
    return jnp.where(low, table, swapped), jnp.where(low, -swapped, table)


def turned(rows, cosine, sine):
    x = rows.astype(jnp.float32)
    return (x * cosine + pltpu.roll(x, HEAD_SIZE // 2, 1) * sine).astype(jnp.bfloat16)


def kernel(
    shape, q_in, k_in, v_in, table_in, out,
    q_raw, q_rot, kv, k_rot, s_buf, w_buf, table, table_next, table_far, peak, total, acc, o_buf,
    local_sem, pair_send, pair_recv, slot_recv, chain_send, flat_send, relay_send,
    out_local, out_send, out_recv,
):
    shard, pairs, side_a, side_b, sequences, span = shape
    rows = 2 * shard
    length = pairs * rows
    s = lax.axis_index("seq")
    g = lax.axis_index("stretch")
    h = s % 2
    p = s // 2
    a = p // side_b
    b = p % side_b
    n = g // sequences
    partner = {"seq": s + 1 - 2 * h}

    def block_at(shift):
        return {"stretch": g + shift * sequences}

    mesh_type = pl.DeviceIdType.MESH

    def pair_at(a_index, b_index):
        return a_index * side_b + b_index

    def device_at(pair):
        return {"seq": 2 * pair + h}

    a_peers = [pair_at((a + j) % side_a, b) for j in range(1, side_a)]
    b_peers = [pair_at(a, (b + j) % side_b) for j in range(1, side_b)]
    diagonal = [
        pair_at((a + i) % side_a, (b + j) % side_b)
        for i in range(1, side_a)
        for j in range(1, side_b)
    ]

    def at(start, size, unit):
        return pl.ds(pl.multiple_of(start, unit), size)

    mine = at(h * shard, shard, shard)
    own_rows = at(p * rows + h * shard, shard, shard)

    def head_columns(head):
        return at(head * HEAD_SIZE, HEAD_SIZE, HEAD_SIZE)

    local = [
        (k_in.at[:, head_columns(h)], kv.at[0, 0, own_rows, :]),
        (v_in.at[:, head_columns(h)], kv.at[1, 0, own_rows, :]),
        (q_in.at[:, at(h * WIDTH, WIDTH, HEAD_SIZE)], q_raw.at[mine, :]),
        (table_in.at[pl.ds(0, length), :], table),
        (table_in.at[at(length + p * rows, rows, rows), :], table_next),
        (table_in.at[pl.ds(2 * length - 8, 8), :], table_far),
    ]
    local = [
        pltpu.make_async_copy(src, dst, local_sem.at[i]) for i, (src, dst) in enumerate(local)
    ]
    for copy in local:
        copy.start()

    barrier = pltpu.get_barrier_semaphore()

    def greet(device):
        pl.semaphore_signal(barrier, inc=1, device_id=device, device_id_type=mesh_type)

    greet(partner)
    for peer in a_peers + b_peers:
        greet(device_at(peer))

    for k in range(1, BLOCKS):
        @pl.when(n + k < BLOCKS)
        def _():
            greet(block_at(k))

        @pl.when(n >= k)
        def _():
            greet(block_at(-k))

    pl.semaphore_wait(barrier, len(a_peers) + len(b_peers) + BLOCKS)

    swap = [
        (k_in.at[:, head_columns(1 - h)], kv.at[0, 0, own_rows, :]),
        (v_in.at[:, head_columns(1 - h)], kv.at[1, 0, own_rows, :]),
        (q_in.at[:, at((1 - h) * WIDTH, WIDTH, HEAD_SIZE)], q_raw.at[mine, :]),
    ]
    swap = [
        pltpu.make_async_remote_copy(
            src_ref=src, dst_ref=dst, send_sem=pair_send.at[i], recv_sem=pair_recv.at[i],
            device_id=partner, device_id_type=mesh_type,
        )
        for i, (src, dst) in enumerate(swap)
    ]
    for copy in swap:
        copy.start()

    def slot(t, d, pair):
        return kv.at[t, d, at(pair * rows, rows, rows), :]

    def message(t, d, pair, device, d_to, send_sem):
        return pltpu.make_async_remote_copy(
            src_ref=slot(t, d, pair), dst_ref=slot(t, d_to, pair),
            send_sem=send_sem, recv_sem=slot_recv.at[t, d_to, pair],
            device_id=device, device_id_type=mesh_type,
        )

    def arrived(t, d, pair):
        message(t, d, pair, partner, d, chain_send.at[0, 0]).wait_recv()

    def lift(t, k):
        return message(t, 0, p, block_at(k), k, chain_send.at[t, k])

    def flat(t, d):
        return [
            message(t, d, p, device_at(peer), d, flat_send.at[t, d, i])
            for i, peer in enumerate(b_peers + a_peers)
        ]

    def relays(t, d):
        sources, targets = (b_peers, a_peers) if t == 0 else (a_peers, b_peers)
        return [
            [
                message(t, d, source, device_at(target), d, relay_send.at[t, d, i, j])
                for j, target in enumerate(targets)
            ]
            for i, source in enumerate(sources)
        ]

    def column(d, first):
        for t in range(2):
            if first:
                local[t].wait()
                swap[t].wait_recv()
            else:
                arrived(t, d, p)

            if first:
                for k in range(BLOCKS - 1, 0, -1):
                    @pl.when(n + k < BLOCKS)
                    def _():
                        lift(t, k).start()

            for copy in flat(t, d):
                copy.start()

    def spread(d):
        for t, sources in ((0, b_peers), (1, a_peers)):
            for source, copies in zip(sources, relays(t, d)):
                arrived(t, d, source)
                for copy in copies:
                    copy.start()
        for t, sources in ((1, b_peers), (0, a_peers)):
            for source in sources:
                arrived(t, d, source)

    def settle(d):
        for t in range(2):
            for source in diagonal:
                arrived(t, d, source)

    def rotate_queries(version, cosine, sine):
        for c in range(CLUSTER):
            q_rot[version, c] = turned(
                q_raw[:, c * HEAD_SIZE : (c + 1) * HEAD_SIZE], cosine, sine
            )

    def attend(d, line, causal):
        where = at(line * span, span, span)
        version = jnp.minimum(d, 2)
        for i in range(side_b):
            tile = at(line * span + i * rows, rows, rows)
            cosine, sine = factors(table[tile, :])
            k_rot[i * rows : (i + 1) * rows, :] = turned(kv[0, d, tile, :], cosine, sine)

        def score(c):
            s_buf[c % 2] = lax.dot_general(
                q_rot[version, c], k_rot[...], (((1,), (1,)), ((), ())),
                preferred_element_type=jnp.float32,
            )

        score(0)
        for c in range(CLUSTER):
            if c + 1 < CLUSTER:
                score(c + 1)
            for start in range(0, rows, 64):
                sub = slice(start, start + 64)
                scores = s_buf[c % 2, sub, :]
                if causal:
                    row = b * rows + start + lax.broadcasted_iota(jnp.int32, scores.shape, 0)
                    key = lax.broadcasted_iota(jnp.int32, scores.shape, 1)
                    scores = jnp.where(row >= key, scores, -1e30)
                new = jnp.max(scores, axis=1, keepdims=True) * SCALE
                if not causal:
                    old = peak[c, sub, :]
                    new = jnp.maximum(old, new)
                    fade = jnp.exp2(old - new)
                    peak[c, sub, :] = new
                    new = new[:, :1]
                else:
                    peak[c, sub, :] = jnp.broadcast_to(new, (64, HEAD_SIZE))
                weights = jnp.exp2(scores * SCALE - new)
                part = weights[:, :HEAD_SIZE]
                for i in range(1, span // HEAD_SIZE):
                    part = part + weights[:, i * HEAD_SIZE : (i + 1) * HEAD_SIZE]
                if causal:
                    total[c, sub, :] = part
                else:
                    total[c, sub, :] = total[c, sub, :] * fade + part
                    acc[c, sub, :] = acc[c, sub, :] * fade
                w_buf[c % 2, sub, :] = weights.astype(jnp.bfloat16)
            product = jnp.dot(
                w_buf[c % 2], kv[1, d, where, :], preferred_element_type=jnp.float32
            )
            acc[c] = product if causal else acc[c] + product

    column(0, True)
    for copy in local[2:]:
        copy.wait()
    swap[2].wait_recv()
    rotate_queries(0, *factors(table[at(p * rows, rows, rows), :]))
    rotate_queries(1, *factors(table_next[...]))
    cosine, sine = factors(table_far[...])
    rotate_queries(
        2,
        jnp.broadcast_to(cosine[7:8], (rows, HEAD_SIZE)),
        jnp.broadcast_to(sine[7:8], (rows, HEAD_SIZE)),
    )
    spread(0)

    @pl.when(n > 0)
    def _():
        column(1, False)

    attend(0, a, True)
    def block(d, carry):
        @pl.when(d + 1 <= n)
        def _():
            spread(d + 1)

        @pl.when(d + 2 <= n)
        def _():
            column(d + 2, False)

        settle(d)

        def visit(i, inner):
            line = (a + i) % side_a
            ahead = d + i // side_a

            @pl.when((ahead <= n) & ((d > 0) | (i == side_a) | (line < a)))
            def _():
                attend(ahead, line, False)

            return inner

        lax.fori_loop(1, side_a + 1, visit, 0)
        return carry

    lax.fori_loop(0, n + 1, block, 0)

    theirs = at((1 - h) * shard, shard, shard)

    def results(c):
        where = head_columns(h * CLUSTER + c)
        return (
            pltpu.make_async_copy(o_buf.at[c, mine, :], out.at[:, where], out_local.at[c]),
            pltpu.make_async_remote_copy(
                src_ref=o_buf.at[c, theirs, :], dst_ref=out.at[:, where],
                send_sem=out_send.at[c], recv_sem=out_recv.at[c],
                device_id=partner, device_id_type=mesh_type,
            ),
        )

    for c in range(CLUSTER + 1):
        if c < CLUSTER:
            under = jnp.sum(total[c], axis=1, keepdims=True)
            o_buf[c] = (acc[c] / under).astype(jnp.bfloat16)
        if c > 0:
            for copy in results(c - 1):
                copy.start()

    for copy in swap:
        copy.wait_send()

    def sent(d, carry):
        for t in range(2):
            for copy in flat(t, d):
                copy.wait_send()
            for copies in relays(t, d):
                for copy in copies:
                    copy.wait_send()
        return carry

    lax.fori_loop(0, n + 1, sent, 0)
    for t in range(2):
        for k in range(1, BLOCKS):
            @pl.when(n + k < BLOCKS)
            def _():
                lift(t, k).wait_send()

    for c in range(CLUSTER):
        here, there = results(c)
        here.wait()
        there.wait_send()
        there.wait_recv()


def on_device(queries, keys, values):
    shard = queries.shape[0]
    pairs = lax.axis_size("seq") // 2
    sequences = lax.axis_size("stretch") // BLOCKS
    side_a = max(i for i in range(1, pairs + 1) if pairs % i == 0 and i * i <= pairs)
    side_b = pairs // side_a
    rows = 2 * shard
    length = pairs * rows
    span = side_b * rows
    shape = (shard, pairs, side_a, side_b, sequences, span)
    table = jnp.asarray(rotary_table(2 * length))
    dma = pltpu.SemaphoreType.DMA
    peers = max(side_a - 1 + side_b - 1, 1)
    most = max(side_b - 1, side_a - 1, 1)
    return pl.pallas_call(
        functools.partial(kernel, shape),
        out_shape=jax.ShapeDtypeStruct(queries.shape, jnp.bfloat16),
        in_specs=[pl.BlockSpec(memory_space=pl.ANY)] * 4,
        out_specs=pl.BlockSpec(memory_space=pl.ANY),
        scratch_shapes=[
            pltpu.VMEM((rows, WIDTH), jnp.bfloat16),
            pltpu.VMEM((3, CLUSTER, rows, HEAD_SIZE), jnp.bfloat16),
            pltpu.VMEM((2, BLOCKS, length, HEAD_SIZE), jnp.bfloat16),
            pltpu.VMEM((span, HEAD_SIZE), jnp.bfloat16),
            pltpu.VMEM((2, rows, span), jnp.float32),
            pltpu.VMEM((2, rows, span), jnp.bfloat16),
            pltpu.VMEM((length, HEAD_SIZE), jnp.float32),
            pltpu.VMEM((rows, HEAD_SIZE), jnp.float32),
            pltpu.VMEM((8, HEAD_SIZE), jnp.float32),
            pltpu.VMEM((CLUSTER, rows, HEAD_SIZE), jnp.float32),
            pltpu.VMEM((CLUSTER, rows, HEAD_SIZE), jnp.float32),
            pltpu.VMEM((CLUSTER, rows, HEAD_SIZE), jnp.float32),
            pltpu.VMEM((CLUSTER, rows, HEAD_SIZE), jnp.bfloat16),
            dma((6,)),
            dma((3,)),
            dma((3,)),
            dma((2, BLOCKS, pairs)),
            dma((2, BLOCKS)),
            dma((2, BLOCKS, peers)),
            dma((2, BLOCKS, most, most)),
            dma((CLUSTER,)),
            dma((CLUSTER,)),
            dma((CLUSTER,)),
        ],
        compiler_params=pltpu.CompilerParams(
            collective_id=0, has_side_effects=True, vmem_limit_bytes=60 * 1024 * 1024
        ),
    )(queries, keys, values, table)


def solution(mesh):
    placed = P(("stretch", "seq"), None)
    return jax.shard_map(
        on_device, mesh=mesh, in_specs=(placed,) * 3, out_specs=placed, check_vma=False
    )
```

profile of v0, /device:TPU:25, one launch (start us, length us, event | category | flops | bytes accessed | tf_op | source)
XLA Modules:
  0.0 38.7 jit_solution(2031572643587032325)
XLA Ops:
  0.0 36.9 %shard_map.46 = bf16[128,1792]{1,0:T(8,128)(2,1)} custom-call(bf16[128,1792]{1,0:T(8,128)(2,1)} %q_in.1, bf16[128,256]{1,0:T(8,128)(2,1)} %k_in.1, bf16[128,256]{1,0:T(8,128)(2,1)} %v_in.1, f32[2048,128]{1,0:T(8,128)} %constant.2.clone.table_in), custom_call_target="tpu_custom_call" | custom-call | tf_op jit(solution)/shard_map/pallas_call | solution.py:360
  36.9 1.8 %copy.6 = bf16[128,1792]{1,0:T(8,128)(2,1)} copy(bf16[128,1792]{1,0:T(8,128)(2,1)} %shard_map.46) | data formatting | bytes 917504
where the time goes:
time: 39.1 us; the launch traced here: 38.7 us
  Pallas kernels  36.9 us (94%)
  local copies, waits for them, and re-layouts  1.82 us (5%)
    pallas_call x1, Pallas kernels, on_device(): pl.pallas_call(functools.partial(kernel, shape), out_shape=jax.ShapeDtype...  36.9 us
    unnamed x1, local copies, waits for them, and re-layouts  1.82 us

commit v1 on v0

v1 whole, which is shorter than its diff:
```python
import functools
import math

import jax
import jax.numpy as jnp
import numpy as np
from jax import lax
from jax.experimental import pallas as pl
from jax.experimental.pallas import tpu as pltpu
from jax.sharding import PartitionSpec as P

QUERY_HEADS = 14
KEY_VALUE_HEADS = 2
HEAD_SIZE = 128
BLOCKS = 4
CLUSTER = QUERY_HEADS // KEY_VALUE_HEADS
WIDTH = CLUSTER * HEAD_SIZE
HALF = HEAD_SIZE // 2
SCALE = math.log2(math.e) / math.sqrt(HEAD_SIZE)
MASKED = -1e30


def rotary_table(positions):
    inverse = 10000000.0 ** (-(np.arange(HALF, dtype=np.float64) * 2.0) / HEAD_SIZE)
    angles = np.arange(positions, dtype=np.float64)[:, None] * inverse[None, :]
    return np.concatenate([np.cos(angles), np.sin(angles)], axis=1).astype(np.float32)


def turned_rows(rows, table):
    swapped = pltpu.roll(table, HALF, 1)
    low = lax.broadcasted_iota(jnp.int32, table.shape, 1) < HALF
    cosine, sine = jnp.where(low, table, swapped), jnp.where(low, -swapped, table)
    x = rows.astype(jnp.float32)
    return (x * cosine + pltpu.roll(x, HALF, 1) * sine).astype(jnp.bfloat16)


def turned_columns(columns, table):
    x, y = columns[:HALF], columns[HALF:]
    cosine, sine = table[:HALF], table[HALF:]
    return jnp.concatenate([x * cosine - y * sine, y * cosine + x * sine], axis=0).astype(
        jnp.bfloat16
    )


def kernel(
    shape, q_in, k_in, v_in, rows_in, columns_in, far_in, out,
    q_own, q_swap, k_own, v_own, k_send, v_send, k_buf, v_buf, q_rot,
    s_even, s_odd, w_even, w_odd, row_table, near_table, next_table, far_table,
    peak, total, fade, top, acc, o_buf,
    local_sem, swap_send, swap_recv, slot_recv, first_send, flat_send, relay_send, lift_send,
    out_local, out_send, out_recv,
):
    shard, pairs, side_a, side_b, sequences, span = shape
    rows = 2 * shard
    length = pairs * rows
    s = lax.axis_index("seq")
    g = lax.axis_index("stretch")
    h = s % 2
    p = s // 2
    a = p // side_b
    b = p % side_b
    n = g // sequences
    last = BLOCKS - 1
    partner = {"seq": s + 1 - 2 * h}
    mesh_type = pl.DeviceIdType.MESH

    def pair_at(a_index, b_index):
        return a_index * side_b + b_index

    def device_at(pair, core):
        return {"seq": 2 * pair + core}

    def block_at(shift, core):
        return {"seq": 2 * p + core, "stretch": g + shift * sequences}

    a_peers = [pair_at((a + i) % side_a, b) for i in range(1, side_a)]
    b_peers = [pair_at(a, (b + j) % side_b) for j in range(1, side_b)]
    diagonal = [
        pair_at((a + i) % side_a, (b + j) % side_b)
        for i in range(1, side_a)
        for j in range(1, side_b)
    ]

    def at(start, size, unit):
        return pl.ds(pl.multiple_of(start, unit), size)

    def head_columns(head):
        return at(head * HEAD_SIZE, HEAD_SIZE, HEAD_SIZE)

    def own_columns(core):
        return at(core * WIDTH, WIDTH, HEAD_SIZE)

    def half_columns(core):
        return at(core * shard, shard, shard)

    mine = half_columns(h)
    theirs = half_columns(1 - h)

    local = [
        (k_in, k_own),
        (rows_in.at[at(p * rows + h * shard, shard, shard), :], row_table),
        (v_in, v_own),
        (q_in, q_own),
        (columns_in.at[:, at(p * rows, rows, rows)], near_table),
        (columns_in.at[:, at(length + p * rows, rows, rows)], next_table),
        (far_in, far_table),
    ]
    local = [
        pltpu.make_async_copy(src, dst, local_sem.at[i]) for i, (src, dst) in enumerate(local)
    ]
    for copy in local:
        copy.start()

    barrier = pltpu.get_barrier_semaphore()

    def greet(device):
        pl.semaphore_signal(barrier, inc=1, device_id=device, device_id_type=mesh_type)

    for core in range(2):
        @pl.when(n < last)
        def _():
            greet(block_at(1, core))

        @pl.when(n > 0)
        def _():
            greet(block_at(-1, core))

        @pl.when(n == 0)
        def _():
            greet(block_at(last, core))

        @pl.when(n == last)
        def _():
            greet(block_at(-last, core))

        for peer in a_peers + b_peers:
            greet(device_at(peer, core))
    greet(partner)

    def rotate_queries(source, half):
        near, later, far = near_table[:, half], next_table[:, half], far_table[:, :1]
        for c in range(CLUSTER):
            x = source(c).T.astype(jnp.float32)
            q_rot[0, c, :, half] = turned_columns(x, near)
            q_rot[1, c, :, half] = turned_columns(x, later)
            q_rot[2, c, :, half] = turned_columns(x, far)

    local[0].wait()
    local[1].wait()
    local[2].wait()
    for head in range(KEY_VALUE_HEADS):
        columns = slice(head * HEAD_SIZE, (head + 1) * HEAD_SIZE)
        k_send[head] = turned_rows(k_own[:, columns], row_table[...])
        v_send[head] = v_own[:, columns].T
    k_buf[0, at(p * rows + h * shard, shard, shard), :] = k_send[h]
    v_buf[0, p, h] = v_send[h]
    for copy in local[3:]:
        copy.wait()
    rotate_queries(lambda c: q_own[:, at(h * WIDTH + c * HEAD_SIZE, HEAD_SIZE, HEAD_SIZE)], mine)

    pl.semaphore_wait(barrier, 1 + 2 * (len(a_peers) + len(b_peers)) + 4)

    def slot(t, d, pair):
        if t == 0:
            return k_buf.at[d, at(pair * rows, rows, rows), :]
        return v_buf.at[d, pair]

    def part(t, d, pair, core):
        if t == 0:
            return k_buf.at[d, at(pair * rows + core * shard, shard, shard), :]
        return v_buf.at[d, pair, core]

    def message(t, d, pair, device, d_to, send_sem):
        return pltpu.make_async_remote_copy(
            src_ref=slot(t, d, pair), dst_ref=slot(t, d_to, pair),
            send_sem=send_sem, recv_sem=slot_recv.at[t, d_to, pair],
            device_id=device, device_id_type=mesh_type,
        )

    def first(t, core, device, d_to, i):
        return pltpu.make_async_remote_copy(
            src_ref=(k_send, v_send)[t].at[core], dst_ref=part(t, d_to, p, h),
            send_sem=first_send.at[t, core, i], recv_sem=slot_recv.at[t, d_to, p],
            device_id=device, device_id_type=mesh_type,
        )

    def arrived(t, d, pair):
        message(t, d, pair, partner, d, lift_send.at[0, 0, 0, 0]).wait_recv()

    def routes(t, d):
        if d == 0:
            found = [(n < last, 1, 1), (n == 0, last, last)]
            return found + [(n == 1, -1, last)] if t == 1 else found
        if d == 1:
            return [((n == 1) if t == 1 else (n == 1) | (n == 2), 1, 2)]
        return [(n == 0, last, 2)] if d == last and t == 1 else []

    def firsts(t):
        peers = a_peers + b_peers
        plain = [
            first(t, core, device_at(peer, core), 0, i)
            for i, peer in enumerate(peers)
            for core in range(2)
        ]
        lifted = [
            (when, first(t, core, block_at(shift, core), d_to, len(peers) + i))
            for i, (when, shift, d_to) in enumerate(routes(t, 0))
            for core in range(2)
        ]
        own = pltpu.make_async_remote_copy(
            src_ref=(k_send, v_send)[t].at[1 - h], dst_ref=part(t, 0, p, h),
            send_sem=swap_send.at[t], recv_sem=swap_recv.at[t],
            device_id=partner, device_id_type=mesh_type,
        )
        return own, plain, lifted

    query_swap = pltpu.make_async_remote_copy(
        src_ref=q_own.at[:, own_columns(1 - h)], dst_ref=q_swap,
        send_sem=swap_send.at[2], recv_sem=swap_recv.at[2],
        device_id=partner, device_id_type=mesh_type,
    )

    for t in range(2):
        own, plain, lifted = firsts(t)
        for copy in plain:
            copy.start()
        for when, copy in lifted:
            pl.when(when)(copy.start)
        own.start()
    query_swap.start()

    def flat(t, d):
        return [
            message(t, d, p, device_at(peer, h), d, flat_send.at[t, d, i])
            for i, peer in enumerate(b_peers + a_peers)
        ]

    def relays(t):
        sources, targets = (b_peers, a_peers) if t == 0 else (a_peers, b_peers)
        return [
            [
                message(t, 0, source, device_at(target, h), 0, relay_send.at[t, i, j])
                for j, target in enumerate(targets)
            ]
            for i, source in enumerate(sources)
        ]

    def lifts(t, d, pair, i):
        return [
            (when, message(t, d, pair, block_at(shift, h), d_to, lift_send.at[t, d, i, k]))
            for k, (when, shift, d_to) in enumerate(routes(t, d))
        ]

    def lift(t, d, pair, i):
        for when, copy in lifts(t, d, pair, i):
            pl.when(when)(copy.start)

    def column(t, d):
        arrived(t, d, p)
        for copy in flat(t, d):
            copy.start()
        lift(t, d, p, 0)

    def scores(c, d, line, version, causal, into, side):
        found = jnp.dot(
            k_buf[d, at(line * span, span, span), :], q_rot[version, c],
            preferred_element_type=jnp.float32,
        )
        if causal:
            key = lax.broadcasted_iota(jnp.int32, found.shape, 0)
            row = b * rows + lax.broadcasted_iota(jnp.int32, found.shape, 1)
            found = jnp.where(row >= key, found, MASKED)
        into[...] = found
        top[side] = jnp.max(found.reshape(span // 8, 8, rows), axis=0)

    def weigh(c, causal, source, into, side):
        new = jnp.max(top[side], axis=0, keepdims=True) * SCALE
        if causal:
            new = jnp.broadcast_to(new, (8, rows))
        else:
            old = peak[c]
            new = jnp.maximum(old, new)
            fade[side] = jnp.exp2(old - new)
        peak[c] = new
        new = new[:1]
        added = None
        for start in range(0, span, 64):
            weights = jnp.exp2(source[start : start + 64, :] * SCALE - new)
            some = jnp.sum(weights.reshape(8, 8, rows), axis=0)
            added = some if added is None else added + some
            into[start : start + 64, :] = weights.astype(jnp.bfloat16)
        total[c] = added if causal else total[c] * fade[side] + added

    def gather(c, d, line, causal, source, side):
        values = jnp.concatenate(
            [v_buf[d, line * side_b + i // 2, i % 2] for i in range(2 * side_b)], axis=1
        )
        product = jnp.dot(values, source[...], preferred_element_type=jnp.float32)
        acc[c] = product if causal else acc[c] * fade[side][:1] + product

    def attend(d, line, causal):
        version = jnp.minimum(d, 2)
        s_buf, w_buf = (s_even, s_odd), (w_even, w_odd)
        scores(0, d, line, version, causal, s_buf[0], 0)
        for c in range(CLUSTER):
            if c + 1 < CLUSTER:
                scores(c + 1, d, line, version, causal, s_buf[(c + 1) % 2], (c + 1) % 2)
            if c > 0:
                gather(c - 1, d, line, causal, w_buf[(c - 1) % 2], (c - 1) % 2)
            weigh(c, causal, s_buf[c % 2], w_buf[c % 2], c % 2)
        gather(CLUSTER - 1, d, line, causal, w_buf[(CLUSTER - 1) % 2], (CLUSTER - 1) % 2)

    query_swap.wait_recv()
    rotate_queries(lambda c: q_swap[:, c * HEAD_SIZE : (c + 1) * HEAD_SIZE], theirs)
    for t in range(2):
        pltpu.make_async_remote_copy(
            src_ref=(k_send, v_send)[t].at[h], dst_ref=part(t, 0, p, 1 - h),
            send_sem=swap_send.at[t], recv_sem=swap_recv.at[t],
            device_id=partner, device_id_type=mesh_type,
        ).wait_recv()

    for t, sources in ((0, b_peers), (1, a_peers)):
        for source, copies in zip(sources, relays(t)):
            arrived(t, 0, source)
            for copy in copies:
                copy.start()

        @pl.when(n > 0)
        def _():
            column(t, 1)

        @pl.when(n == last)
        def _():
            column(t, last)

    @pl.when(n == 0)
    def _():
        arrived(1, last, p)
        lift(1, last, p, 0)

    for source in b_peers:
        arrived(1, 0, source)
    attend(0, a, True)

    def visit(j, carry):
        i = j % side_a
        place = j // side_a
        d = jnp.where(place < 2, place, jnp.where((n == last) & (place == 2), last, 2))
        line = (a + i) % side_a

        for t in range(2):
            @pl.when((j == 1 + t) & (n >= 2))
            def _():
                column(t, 2)

        for t in range(2):
            @pl.when(i == 0)
            def _():
                for source in b_peers:
                    arrived(t, d, source)

            for shift in range(1, side_a):
                @pl.when(i == shift)
                def _():
                    there = (a + shift) % side_a

                    @pl.when((t == 0) | (d > 0))
                    def _():
                        arrived(t, d, pair_at(there, b))

                    for k in range(1, side_b):
                        pair = pair_at(there, (b + k) % side_b)
                        arrived(t, d, pair)
                        for level in range(2):
                            @pl.when(d == level)
                            def _():
                                lift(t, level, pair, 1 + (shift - 1) * (side_b - 1) + k - 1)

        @pl.when((d > 0) | (line < a))
        def _():
            attend(d, line, False)

        return carry

    lax.fori_loop(1, side_a * (n + 1), visit, 0)

    @pl.when(n == 0)
    def _():
        for i, pair in enumerate(diagonal):
            arrived(1, last, pair)
            lift(1, last, pair, 1 + i)

    def results(c):
        where = head_columns(h * CLUSTER + c)
        return (
            pltpu.make_async_copy(o_buf.at[c, mine, :], out.at[:, where], out_local.at[c]),
            pltpu.make_async_remote_copy(
                src_ref=o_buf.at[c, theirs, :], dst_ref=out.at[:, where],
                send_sem=out_send.at[c], recv_sem=out_recv.at[c],
                device_id=partner, device_id_type=mesh_type,
            ),
        )

    for c in range(CLUSTER + 1):
        if c < CLUSTER:
            share = 1.0 / jnp.sum(total[c], axis=0, keepdims=True)
            o_buf[c] = (acc[c] * share).astype(jnp.bfloat16).T
        if c > 0:
            for copy in results(c - 1):
                copy.start()

    query_swap.wait_send()
    for t in range(2):
        own, plain, lifted = firsts(t)
        own.wait_send()
        for copy in plain:
            copy.wait_send()
        for when, copy in lifted:
            pl.when(when)(copy.wait_send)
        for copies in relays(t):
            for copy in copies:
                copy.wait_send()

    for t in range(2):
        for d in range(1, BLOCKS):
            @pl.when(d <= n)
            def _():
                for copy in flat(t, d):
                    copy.wait_send()
        for d in range(BLOCKS):
            for i, pair in enumerate([p] + diagonal):
                if d > 0 or i > 0:
                    for when, copy in lifts(t, d, pair, i):
                        pl.when(when)(copy.wait_send)

    for c in range(CLUSTER):
        here, there = results(c)
        here.wait()
        there.wait_send()
        there.wait_recv()


def on_device(queries, keys, values):
    shard = queries.shape[0]
    pairs = lax.axis_size("seq") // 2
    sequences = lax.axis_size("stretch") // BLOCKS
    side_a = max(i for i in range(1, pairs + 1) if pairs % i == 0 and i * i <= pairs)
    side_b = pairs // side_a
    rows = 2 * shard
    length = pairs * rows
    span = side_b * rows
    shape = (shard, pairs, side_a, side_b, sequences, span)
    table = rotary_table(2 * length)
    far = np.broadcast_to(table[-1][:, None], (HEAD_SIZE, HEAD_SIZE))
    dma = pltpu.SemaphoreType.DMA
    peers = max(side_a - 1 + side_b - 1, 1)
    most = max(side_b - 1, side_a - 1, 1)
    lifted = 1 + (side_a - 1) * (side_b - 1)
    bf16, f32 = jnp.bfloat16, jnp.float32
    return pl.pallas_call(
        functools.partial(kernel, shape),
        out_shape=jax.ShapeDtypeStruct(queries.shape, bf16),
        in_specs=[pl.BlockSpec(memory_space=pl.ANY)] * 6,
        out_specs=pl.BlockSpec(memory_space=pl.ANY),
        scratch_shapes=[
            pltpu.VMEM((shard, 2 * WIDTH), bf16),
            pltpu.VMEM((shard, WIDTH), bf16),
            pltpu.VMEM((shard, 2 * HEAD_SIZE), bf16),
            pltpu.VMEM((shard, 2 * HEAD_SIZE), bf16),
            pltpu.VMEM((2, shard, HEAD_SIZE), bf16),
            pltpu.VMEM((2, HEAD_SIZE, shard), bf16),
            pltpu.VMEM((BLOCKS, length, HEAD_SIZE), bf16),
            pltpu.VMEM((BLOCKS, pairs, 2, HEAD_SIZE, shard), bf16),
            pltpu.VMEM((3, CLUSTER, HEAD_SIZE, rows), bf16),
            pltpu.VMEM((span, rows), f32),
            pltpu.VMEM((span, rows), f32),
            pltpu.VMEM((span, rows), bf16),
            pltpu.VMEM((span, rows), bf16),
            pltpu.VMEM((shard, HEAD_SIZE), f32),
            pltpu.VMEM((HEAD_SIZE, rows), f32),
            pltpu.VMEM((HEAD_SIZE, rows), f32),
            pltpu.VMEM((HEAD_SIZE, HEAD_SIZE), f32),
            pltpu.VMEM((CLUSTER, 8, rows), f32),
            pltpu.VMEM((CLUSTER, 8, rows), f32),
            pltpu.VMEM((2, 8, rows), f32),
            pltpu.VMEM((2, 8, rows), f32),
            pltpu.VMEM((CLUSTER, HEAD_SIZE, rows), f32),
            pltpu.VMEM((CLUSTER, rows, HEAD_SIZE), bf16),
            dma((7,)),
            dma((3,)),
            dma((3,)),
            dma((2, BLOCKS, pairs)),
            dma((2, 2, peers + 3)),
            dma((2, BLOCKS, peers)),
            dma((2, most, most)),
            dma((2, BLOCKS, lifted, 3)),
            dma((CLUSTER,)),
            dma((CLUSTER,)),
            dma((CLUSTER,)),
        ],
        compiler_params=pltpu.CompilerParams(
            collective_id=0, has_side_effects=True, vmem_limit_bytes=60 * 1024 * 1024
        ),
    )(
        queries, keys, values,
        jnp.asarray(table[:length]), jnp.asarray(np.ascontiguousarray(table.T)), jnp.asarray(far),
    )


def solution(mesh):
    placed = P(("stretch", "seq"), None)
    return jax.shard_map(
        on_device, mesh=mesh, in_specs=(placed,) * 3, out_specs=placed, check_vma=False
    )
```

time: 39.1 us -> 36.3 us (0.928)
  Pallas kernels: 36.9 us -> 33 us
  local copies, waits for them, and re-layouts: 1.82 us -> 3.18 us
    pallas_call x1, Pallas kernels: 36.9 us -> 33 us  [on_device(): pl.pallas_call(functools.partial(kernel, shape), out_shape=jax.ShapeDtype...]
    another operation x0 -> x1, local copies, waits for them, and re-layouts: none -> 1.37 us
where the time goes in v1:
time: 36.3 us; the launch traced here: 36.1 us
  Pallas kernels  33 us (91%)
  local copies, waits for them, and re-layouts  3.18 us (9%)
    pallas_call x1, Pallas kernels, on_device(): pl.pallas_call(functools.partial(kernel, shape), out_shape=jax.ShapeDtype...  33 us
    unnamed x1, local copies, waits for them, and re-layouts  1.82 us
    another operation x1, local copies, waits for them, and re-layouts  1.37 us

profile of v1, /device:TPU:25, one launch (start us, length us, event | category | flops | bytes accessed | tf_op | source)
XLA Modules:
  0.0 36.1 jit_solution(3153417453437085744)
XLA Ops:
  0.0 1.4 %jit_solution_.3.far_in = f32[128,128]{1,0:T(8,128)} broadcast(f32[128]{0:T(128)} %constant.8.clone), dimensions={0} | broadcast | bytes 66048 | tf_op jit(solution)
  1.4 33.0 %shard_map.64 = bf16[128,1792]{1,0:T(8,128)(2,1)} custom-call(bf16[128,1792]{1,0:T(8,128)(2,1)} %q_in.1, bf16[128,256]{1,0:T(8,128)(2,1)} %k_in.1, bf16[128,256]{1,0:T(8,128)(2,1)} %v_in.1, f32[1024,128]{1,0:T(8,128)} %constant.6.clone.rows_in, f32[128,2048]{1,0:T(8,128)} %constant.7.clone.columns_in, f32[128,128]{1,0:T(8,128)} %jit_solution_.3.far_in), custom_call_target="tpu_custom_call" | custom-call | tf_op jit(solution)/shard_map/pallas_call | solution.py:460
  34.3 1.8 %copy.8 = bf16[128,1792]{1,0:T(8,128)(2,1)} copy(bf16[128,1792]{1,0:T(8,128)(2,1)} %shard_map.64) | data formatting | bytes 917504

commit v2 on v1

--- a/solution.py
+++ b/solution.py
@@ -187,13 +187,13 @@
     def arrived(t, d, pair):
         message(t, d, pair, partner, d, lift_send.at[0, 0, 0, 0]).wait_recv()
 
-    def routes(t, d):
+    def column_routes(d):
         if d == 0:
-            found = [(n < last, 1, 1), (n == 0, last, last)]
-            return found + [(n == 1, -1, last)] if t == 1 else found
-        if d == 1:
-            return [((n == 1) if t == 1 else (n == 1) | (n == 2), 1, 2)]
-        return [(n == 0, last, 2)] if d == last and t == 1 else []
+            return [(n < last, 1, 1), (n == 0, last, last)]
+        return [((n > 0) & (n < last), 1, 2)] if d == 1 else []
+
+    def diagonal_routes(d):
+        return [(n == last - 1, 1, 1), (n == 0, last, last)] if d == 0 else []
 
     def firsts(t):
         peers = a_peers + b_peers
@@ -204,7 +204,7 @@
         ]
         lifted = [
             (when, first(t, core, block_at(shift, core), d_to, len(peers) + i))
-            for i, (when, shift, d_to) in enumerate(routes(t, 0))
+            for i, (when, shift, d_to) in enumerate(column_routes(0))
             for core in range(2)
         ]
         own = pltpu.make_async_remote_copy(
@@ -235,31 +235,39 @@
             for i, peer in enumerate(b_peers + a_peers)
         ]
 
-    def relays(t):
-        sources, targets = (b_peers, a_peers) if t == 0 else (a_peers, b_peers)
+    def relayed(d):
+        return (d == 0) | (n < last) | (d == 2)
+
+    def relay(t, d, i, source):
         return [
-            [
-                message(t, 0, source, device_at(target, h), 0, relay_send.at[t, i, j])
-                for j, target in enumerate(targets)
-            ]
-            for i, source in enumerate(sources)
+            message(t, d, source, device_at(target, h), d, relay_send.at[t, d, i, j])
+            for j, target in enumerate((a_peers, b_peers)[t])
         ]
 
-    def lifts(t, d, pair, i):
+    def pass_on(t, d):
+        for i, source in enumerate((b_peers, a_peers)[t]):
+            arrived(t, d, source)
+
+            @pl.when(relayed(d))
+            def _():
+                for copy in relay(t, d, i, source):
+                    copy.start()
+
+    def lifts(t, d, pair, i, routes):
         return [
             (when, message(t, d, pair, block_at(shift, h), d_to, lift_send.at[t, d, i, k]))
-            for k, (when, shift, d_to) in enumerate(routes(t, d))
+            for k, (when, shift, d_to) in enumerate(routes)
         ]
 
-    def lift(t, d, pair, i):
-        for when, copy in lifts(t, d, pair, i):
+    def lift(t, d, pair, i, routes):
+        for when, copy in lifts(t, d, pair, i, routes):
             pl.when(when)(copy.start)
 
     def column(t, d):
         arrived(t, d, p)
         for copy in flat(t, d):
             copy.start()
-        lift(t, d, p, 0)
+        lift(t, d, p, 0, column_routes(d))
 
     def scores(c, d, line, version, causal, into, side):
         found = jnp.dot(
@@ -319,76 +327,70 @@
             device_id=partner, device_id_type=mesh_type,
         ).wait_recv()
 
-    for t, sources in ((0, b_peers), (1, a_peers)):
-        for source, copies in zip(sources, relays(t)):
-            arrived(t, 0, source)
-            for copy in copies:
-                copy.start()
+    for t in range(2):
+        pass_on(t, 0)
 
         @pl.when(n > 0)
         def _():
             column(t, 1)
 
-        @pl.when(n == last)
-        def _():
-            column(t, last)
-
-    @pl.when(n == 0)
-    def _():
-        arrived(1, last, p)
-        lift(1, last, p, 0)
-
     for source in b_peers:
         arrived(1, 0, source)
     attend(0, a, True)
 
     def visit(j, carry):
-        i = j % side_a
-        place = j // side_a
-        d = jnp.where(place < 2, place, jnp.where((n == last) & (place == 2), last, 2))
-        line = (a + i) % side_a
-
-        for t in range(2):
-            @pl.when((j == 1 + t) & (n >= 2))
+        many = n >= 2
+        most = n == last
+        d = jnp.where(j < 2, 0, jnp.where((j == 2) | (j == 4), 1, 2))
+        d = jnp.where((j == 3) & (n == 1), 1, d)
+        d = jnp.where(((j == 5) & most) | (j == 7), last, d)
+        across = (j == 1) | (j == 4) | (j > 5) | ((j == 3) & (n == 1)) | ((j == 5) & (n == 2))
+
+        for t, d_in, stage, when in ((0, 2, 1, many), (0, last, 2, most), (1, last, 3, most)):
+            @pl.when((j == stage) & when)
             def _():
-                column(t, 2)
-
-        for t in range(2):
-            @pl.when(i == 0)
+                column(t, d_in)
+
+        @pl.when(jnp.logical_not(across))
+        def _():
+            pass_on(0, d)
+            for source in b_peers:
+                arrived(1, d, source)
+            pass_on(1, d)
+
+        def cross(i, inner):
+            line = (a + i) % side_a
+
+            @pl.when(across)
             def _():
-                for source in b_peers:
-                    arrived(t, d, source)
-
-            for shift in range(1, side_a):
-                @pl.when(i == shift)
-                def _():
-                    there = (a + shift) % side_a
-
-                    @pl.when((t == 0) | (d > 0))
+                for t in range(2):
+                    @pl.when(t == 0)
                     def _():
-                        arrived(t, d, pair_at(there, b))
+                        arrived(t, d, pair_at(line, b))
 
                     for k in range(1, side_b):
-                        pair = pair_at(there, (b + k) % side_b)
+                        pair = pair_at(line, (b + k) % side_b)
                         arrived(t, d, pair)
-                        for level in range(2):
-                            @pl.when(d == level)
-                            def _():
-                                lift(t, level, pair, 1 + (shift - 1) * (side_b - 1) + k - 1)
-
-        @pl.when((d > 0) | (line < a))
-        def _():
-            attend(d, line, False)
-
-        return carry
-
-    lax.fori_loop(1, side_a * (n + 1), visit, 0)
-
-    @pl.when(n == 0)
-    def _():
-        for i, pair in enumerate(diagonal):
-            arrived(1, last, pair)
-            lift(1, last, pair, 1 + i)
+
+                        @pl.when(d == 0)
+                        def _():
+                            lift(t, 0, pair, (i - 1) * (side_b - 1) + k, diagonal_routes(0))
+
+            @pl.when((j == 1) & many & (i == side_a - 1))
+            def _():
+                column(1, 2)
+
+            @pl.when((d > 0) | (line < a))
+            def _():
+                attend(d, line, False)
+
+            return inner
+
+        return lax.fori_loop(
+            jnp.where(across, 1, 0), jnp.where(across, side_a, 1), cross, carry
+        )
+
+    lax.fori_loop(1, 2 * (n + 1), visit, 0)
 
     def results(c):
         where = head_columns(h * CLUSTER + c)
@@ -417,21 +419,26 @@
             copy.wait_send()
         for when, copy in lifted:
             pl.when(when)(copy.wait_send)
-        for copies in relays(t):
-            for copy in copies:
-                copy.wait_send()
 
     for t in range(2):
-        for d in range(1, BLOCKS):
+        for d in range(BLOCKS):
             @pl.when(d <= n)
             def _():
-                for copy in flat(t, d):
-                    copy.wait_send()
-        for d in range(BLOCKS):
-            for i, pair in enumerate([p] + diagonal):
-                if d > 0 or i > 0:
-                    for when, copy in lifts(t, d, pair, i):
+                if d > 0:
+                    for copy in flat(t, d):
+                        copy.wait_send()
+                    for when, copy in lifts(t, d, p, 0, column_routes(d)):
                         pl.when(when)(copy.wait_send)
+
+                @pl.when(relayed(d))
+                def _():
+                    for i, source in enumerate((b_peers, a_peers)[t]):
+                        for copy in relay(t, d, i, source):
+                            copy.wait_send()
+
+        for i, pair in enumerate(diagonal):
+            for when, copy in lifts(t, 0, pair, 1 + i, diagonal_routes(0)):
+                pl.when(when)(copy.wait_send)
 
     for c in range(CLUSTER):
         here, there = results(c)
@@ -490,10 +497,10 @@
             dma((3,)),
             dma((3,)),
             dma((2, BLOCKS, pairs)),
-            dma((2, 2, peers + 3)),
+            dma((2, 2, peers + 2)),
             dma((2, BLOCKS, peers)),
-            dma((2, most, most)),
-            dma((2, BLOCKS, lifted, 3)),
+            dma((2, BLOCKS, most, most)),
+            dma((2, BLOCKS, lifted, 2)),
             dma((CLUSTER,)),
             dma((CLUSTER,)),
             dma((CLUSTER,)),

time: 36.3 us -> 34.5 us (0.950)
  Pallas kernels: 33 us -> 31.2 us
    pallas_call x1, Pallas kernels: 33 us -> 31.2 us  [on_device(): pl.pallas_call(functools.partial(kernel, shape), out_shape=jax.ShapeDtype...]
where the time goes in v2:
time: 34.5 us; the launch traced here: 34.4 us
  Pallas kernels  31.2 us (90%)
  local copies, waits for them, and re-layouts  3.18 us (9%)
    pallas_call x1, Pallas kernels, on_device(): pl.pallas_call(functools.partial(kernel, shape), out_shape=jax.ShapeDtype...  31.2 us
    unnamed x1, local copies, waits for them, and re-layouts  1.82 us
    another operation x1, local copies, waits for them, and re-layouts  1.37 us

profile of v2, /device:TPU:25, one launch (start us, length us, event | category | flops | bytes accessed | tf_op | source)
XLA Modules:
  0.0 34.4 jit_solution(3850183470370105613)
XLA Ops:
  0.0 1.4 %jit_solution_.3.far_in = f32[128,128]{1,0:T(8,128)} broadcast(f32[128]{0:T(128)} %constant.8.clone), dimensions={0} | broadcast | bytes 66048 | tf_op jit(solution)
  1.4 31.2 %shard_map.64 = bf16[128,1792]{1,0:T(8,128)(2,1)} custom-call(bf16[128,1792]{1,0:T(8,128)(2,1)} %q_in.1, bf16[128,256]{1,0:T(8,128)(2,1)} %k_in.1, bf16[128,256]{1,0:T(8,128)(2,1)} %v_in.1, f32[1024,128]{1,0:T(8,128)} %constant.6.clone.rows_in, f32[128,2048]{1,0:T(8,128)} %constant.7.clone.columns_in, f32[128,128]{1,0:T(8,128)} %jit_solution_.3.far_in), custom_call_target="tpu_custom_call" | custom-call | tf_op jit(solution)/shard_map/pallas_call | solution.py:467
  32.5 1.8 %copy.8 = bf16[128,1792]{1,0:T(8,128)(2,1)} copy(bf16[128,1792]{1,0:T(8,128)(2,1)} %shard_map.64) | data formatting | bytes 917504

commit v3 on v2

v3 whole, which is shorter than its diff:
```python
import functools
import math

import jax
import jax.numpy as jnp
import numpy as np
from jax import lax
from jax.experimental import pallas as pl
from jax.experimental.pallas import tpu as pltpu
from jax.sharding import PartitionSpec as P

QUERY_HEADS = 14
KEY_VALUE_HEADS = 2
HEAD_SIZE = 128
BLOCKS = 4
CLUSTER = QUERY_HEADS // KEY_VALUE_HEADS
WIDTH = CLUSTER * HEAD_SIZE
HALF = HEAD_SIZE // 2
SCALE = math.log2(math.e) / math.sqrt(HEAD_SIZE)
MASKED = -1e30


def rotary_table(positions):
    inverse = 10000000.0 ** (-(np.arange(HALF, dtype=np.float64) * 2.0) / HEAD_SIZE)
    angles = np.arange(positions, dtype=np.float64)[:, None] * inverse[None, :]
    return np.concatenate([np.cos(angles), np.sin(angles)], axis=1).astype(np.float32)


def turned_rows(rows, table):
    swapped = pltpu.roll(table, HALF, 1)
    low = lax.broadcasted_iota(jnp.int32, table.shape, 1) < HALF
    cosine, sine = jnp.where(low, table, swapped), jnp.where(low, -swapped, table)
    x = rows.astype(jnp.float32)
    return (x * cosine + pltpu.roll(x, HALF, 1) * sine).astype(jnp.bfloat16)


def turned_columns(columns, table):
    x, y = columns[:HALF], columns[HALF:]
    cosine, sine = table[:HALF], table[HALF:]
    return jnp.concatenate([x * cosine - y * sine, y * cosine + x * sine], axis=0).astype(
        jnp.bfloat16
    )


def kernel(
    shape, q_in, k_in, v_in, rows_in, columns_in, far_in, out,
    q_own, q_swap, k_own, v_own, k_send, v_send, k_buf, v_buf, q_rot,
    s_even, s_odd, w_even, w_odd, row_table, near_tables, far_table,
    peak, total, fade, top, acc, o_buf,
    local_sem, swap_send, swap_recv, sent_sem, column_sem, near_sem, cross_sem, out_sem,
):
    shard, pairs, side_a, side_b, sequences, span = shape
    rows = 2 * shard
    length = pairs * rows
    s = lax.axis_index("seq")
    g = lax.axis_index("stretch")
    h = s % 2
    p = s // 2
    a = p // side_b
    b = p % side_b
    n = g // sequences
    last = BLOCKS - 1
    partner = {"seq": s + 1 - 2 * h}
    mesh_type = pl.DeviceIdType.MESH

    def pair_at(a_index, b_index):
        return a_index * side_b + b_index

    def device_at(pair, core):
        return {"seq": 2 * pair + core}

    def block_at(shift, core):
        return {"seq": 2 * p + core, "stretch": g + shift * sequences}

    a_peers = [pair_at((a + i) % side_a, b) for i in range(1, side_a)]
    b_peers = [pair_at(a, (b + j) % side_b) for j in range(1, side_b)]
    across_a, across_b = len(a_peers), len(b_peers)
    across = across_a * across_b

    def at(start, size, unit):
        return pl.ds(pl.multiple_of(start, unit), size)

    def half_columns(core):
        return at(core * shard, shard, shard)

    mine = half_columns(h)
    theirs = half_columns(1 - h)

    local = [
        (k_in, k_own, 0),
        (rows_in.at[at(p * rows + h * shard, shard, shard), :], row_table, 1),
        (v_in, v_own, 2),
        (q_in, q_own, 3),
        (columns_in.at[:, at(p * rows, rows, rows)], near_tables.at[0], 4),
        (columns_in.at[:, at(length + p * rows, rows, rows)], near_tables.at[1], 4),
        (far_in, far_table, 5),
    ]
    local = [pltpu.make_async_copy(src, dst, local_sem.at[i]) for src, dst, i in local]
    for copy in local:
        copy.start()

    barrier = pltpu.get_barrier_semaphore()

    def greet(device):
        pl.semaphore_signal(barrier, inc=1, device_id=device, device_id_type=mesh_type)

    for core in range(2):
        @pl.when(n < last)
        def _():
            greet(block_at(1, core))

        @pl.when(n > 0)
        def _():
            greet(block_at(-1, core))

        @pl.when((n == 0) | (n == last))
        def _():
            greet(partner)

        for peer in a_peers + b_peers:
            greet(device_at(peer, core))
    greet(partner)

    for copy in local[:3]:
        copy.wait()
    for head in range(KEY_VALUE_HEADS):
        columns = slice(head * HEAD_SIZE, (head + 1) * HEAD_SIZE)
        k_send[head] = turned_rows(k_own[:, columns], row_table[...])
        v_send[head] = v_own[:, columns].T

    def slot(t, d, pair):
        return (k_buf, v_buf)[t].at[pl.ds((d * pairs + pair) * 2, 2)]

    def place(d, pair, core):
        return (d * pairs + pair) * 2 + core

    k_buf[place(0, p, h)] = k_send[h]
    v_buf[place(0, p, h)] = v_send[h]
    local[3].wait()

    pl.semaphore_wait(barrier, 1 + 2 * (across_a + across_b) + 4)

    def send(src, dst, sent, received, device):
        return pltpu.make_async_remote_copy(
            src_ref=src, dst_ref=dst, send_sem=sent, recv_sem=received,
            device_id=device, device_id_type=mesh_type,
        )

    def halves(count):
        return k_buf.at[pl.ds(0, count)]

    def await_slots(count, received):
        some = halves(2 * count)
        send(some, some, swap_send, received, partner).wait_recv()

    def first(t, core, device, d_to, received):
        dst = (k_buf, v_buf)[t].at[place(d_to, p, h)]
        send((k_send, v_send)[t].at[core], dst, sent_sem.at[t, 0], received, device).start()

    def message(t, d, pair, device, d_to, group, received):
        src, dst = slot(t, d, pair), slot(t, d_to, pair)
        send(src, dst, sent_sem.at[t, group], received, device).start()

    def peers(t, d):
        to_a = cross_sem.at[d] if t == 0 else near_sem.at[1, d]
        return [(peer, near_sem.at[t, d]) for peer in b_peers] + [
            (peer, to_a) for peer in a_peers
        ]

    query_swap = send(
        q_own.at[:, at((1 - h) * WIDTH, WIDTH, HEAD_SIZE)], q_swap,
        swap_send, swap_recv.at[1], partner,
    )
    for t in range(2):
        for peer, received in peers(t, 0):
            for core in range(2):
                first(t, core, device_at(peer, core), 0, received)

        @pl.when(n < last)
        def _():
            for core in range(2):
                first(t, core, block_at(1, core), 1, column_sem.at[t, 1])

        first(t, 1 - h, partner, 0, swap_recv.at[0])
    query_swap.start()

    def column(t, d):
        await_slots(1, column_sem.at[t, d])
        for peer, received in peers(t, d):
            message(t, d, p, device_at(peer, h), d, 0, received)

        if not (isinstance(d, int) and d == last):
            @pl.when(n < last)
            def _():
                message(t, d, p, block_at(1, h), d + 1, 0, column_sem.at[t, d + 1])

    def relayed(d):
        return (d == 0) | (n < last) | (d == last)

    def pass_on(t, d):
        sources, targets = ((b_peers, a_peers), (a_peers, b_peers))[t]
        await_slots(across_b + t * across_a, near_sem.at[t, d])

        @pl.when(relayed(d))
        def _():
            for source in sources:
                for target in targets:
                    message(t, d, source, device_at(target, h), d, 1, cross_sem.at[d])

    def pass_up(d):
        for t in range(2):
            for i in range(1, side_a):
                for k in range(1, side_b):
                    pair = pair_at((a + i) % side_a, (b + k) % side_b)
                    message(t, d, pair, block_at(1, h), d + 1, 1, cross_sem.at[d + 1])

    def rotate_queries(source, half):
        near, later, far = near_tables[0, :, half], near_tables[1, :, half], far_table[:, :1]
        for c in range(CLUSTER):
            x = source(c).T.astype(jnp.float32)
            q_rot[0, c, :, half] = turned_columns(x, near)
            q_rot[1, c, :, half] = turned_columns(x, later)
            q_rot[2, c, :, half] = turned_columns(x, far)

    def scores(c, d, line, version, causal, into, side):
        keys = k_buf[pl.ds(place(d, line * side_b, 0), 2 * side_b)].reshape(span, HEAD_SIZE)
        found = jnp.dot(keys, q_rot[version, c], preferred_element_type=jnp.float32)
        if causal:
            key = lax.broadcasted_iota(jnp.int32, found.shape, 0)
            row = b * rows + lax.broadcasted_iota(jnp.int32, found.shape, 1)
            found = jnp.where(row >= key, found, MASKED)
        into[...] = found
        top[side] = jnp.max(found.reshape(span // 8, 8, rows), axis=0)

    def weigh(c, causal, source, into, side):
        new = jnp.max(top[side], axis=0, keepdims=True) * SCALE
        if causal:
            new = jnp.broadcast_to(new, (8, rows))
        else:
            old = peak[c]
            new = jnp.maximum(old, new)
            fade[side] = jnp.exp2(old - new)
        peak[c] = new
        new = new[:1]
        added = None
        for start in range(0, span, 64):
            weights = jnp.exp2(source[start : start + 64, :] * SCALE - new)
            some = jnp.sum(weights.reshape(8, 8, rows), axis=0)
            added = some if added is None else added + some
            into[start : start + 64, :] = weights.astype(jnp.bfloat16)
        total[c] = added if causal else total[c] * fade[side] + added

    def gather(c, d, line, causal, source, side):
        values = jnp.concatenate(
            [v_buf[place(d, line * side_b, i)] for i in range(2 * side_b)], axis=1
        )
        product = jnp.dot(values, source[...], preferred_element_type=jnp.float32)
        acc[c] = product if causal else acc[c] * fade[side][:1] + product

    def result(c):
        where = at((h * CLUSTER + c) * HEAD_SIZE, HEAD_SIZE, HEAD_SIZE)
        return send(
            o_buf.at[c, theirs, :], out.at[:, where], out_sem.at[0], out_sem.at[1], partner
        )

    def finish(c):
        share = 1.0 / jnp.sum(total[c], axis=0, keepdims=True)
        o_buf[c] = (acc[c] * share).astype(jnp.bfloat16).T
        out[:, at((h * CLUSTER + c) * HEAD_SIZE, HEAD_SIZE, HEAD_SIZE)] = o_buf[c, mine, :]

    def attend(d, line, causal, final):
        version = jnp.minimum(d, 2)
        s_buf, w_buf = (s_even, s_odd), (w_even, w_odd)
        scores(0, d, line, version, causal, s_buf[0], 0)
        for c in range(CLUSTER + 1):
            if c + 1 < CLUSTER:
                scores(c + 1, d, line, version, causal, s_buf[(c + 1) % 2], (c + 1) % 2)
            if c > 0:
                gather(c - 1, d, line, causal, w_buf[(c - 1) % 2], (c - 1) % 2)
                if final:
                    finish(c - 1)
                    if c > 1:
                        result(c - 2).start()
            if c < CLUSTER:
                weigh(c, causal, s_buf[c % 2], w_buf[c % 2], c % 2)
        if final:
            result(CLUSTER - 1).start()

    for copy in local[6:]:
        copy.wait()
    pltpu.make_async_copy(near_tables, near_tables, local_sem.at[4]).wait()
    rotate_queries(lambda c: q_own[:, at(h * WIDTH + c * HEAD_SIZE, HEAD_SIZE, HEAD_SIZE)], mine)
    query_swap.wait_recv()
    rotate_queries(lambda c: q_swap[:, c * HEAD_SIZE : (c + 1) * HEAD_SIZE], theirs)
    await_slots(1, swap_recv.at[0])

    for t in range(2):
        pass_on(t, 0)

        @pl.when(n > 0)
        def _():
            column(t, 1)

    attend(0, a, True, False)

    def cross(d):
        await_slots(across_a + 2 * across, cross_sem.at[d])

        @pl.when((n == last - 1) & (d < 2))
        def _():
            pass_up(d)

    def visit(j, carry):
        many = n >= 2
        most = n == last
        d = jnp.where(j < 2, 0, jnp.where((j == 2) | (j == 4), 1, 2))
        d = jnp.where((j == 3) & (n == 1), 1, d)
        d = jnp.where(((j == 5) & most) | (j == 7), last, d)
        other = (j == 1) | (j == 4) | (j > 5) | ((j == 3) & (n == 1)) | ((j == 5) & (n == 2))

        for t, d_in, stage, when in ((0, 2, 1, many), (0, last, 2, most), (1, last, 3, most)):
            @pl.when((j == stage) & when)
            def _():
                column(t, d_in)

        @pl.when(jnp.logical_not(other))
        def _():
            pass_on(0, d)
            pass_on(1, d)

        @pl.when(other)
        def _():
            cross(d)

        @pl.when((j == 1) & many)
        def _():
            column(1, 2)

        def inner(i, inside):
            line = (a + i) % side_a

            @pl.when((d > 0) | (line < a))
            def _():
                attend(d, line, False, False)

            return inside

        ends = jnp.where(other, side_a - jnp.where(j == 2 * n + 1, 1, 0), 1)
        return lax.fori_loop(jnp.where(other, 1, 0), ends, inner, carry)

    lax.fori_loop(1, 2 * (n + 1), visit, 0)
    line = (a + side_a - 1) % side_a
    reached = (n > 0) | (line < a)

    @pl.when(reached)
    def _():
        attend(n, line, False, True)

    @pl.when(jnp.logical_not(reached))
    def _():
        for c in range(CLUSTER + 1):
            if c < CLUSTER:
                finish(c)
            if c > 0:
                result(c - 1).start()

    query_swap.wait_send()
    for k in range(BLOCKS):
        lifted = 2 if k < last else 0
        direct = 2 * (across_a + across_b)
        counts = (
            direct + 1 + lifted + k * (direct + lifted),
            2 * across * (k + 1 if k < last else 2) + (4 * across if k == last - 1 else 0),
        )

        @pl.when(n == k)
        def _():
            for t in range(2):
                for group, count in enumerate(counts):
                    if count:
                        some = halves(count)
                        send(
                            some, some, sent_sem.at[t, group], swap_recv.at[0], partner
                        ).wait_send()

    whole = send(q_swap, q_swap, out_sem.at[0], out_sem.at[1], partner)
    whole.wait_send()
    whole.wait_recv()


def on_device(queries, keys, values):
    shard = queries.shape[0]
    pairs = lax.axis_size("seq") // 2
    sequences = lax.axis_size("stretch") // BLOCKS
    side_a = max(i for i in range(1, pairs + 1) if pairs % i == 0 and i * i <= pairs)
    side_b = pairs // side_a
    rows = 2 * shard
    length = pairs * rows
    span = side_b * rows
    shape = (shard, pairs, side_a, side_b, sequences, span)
    table = rotary_table(2 * length)
    far = np.broadcast_to(table[-1][:, None], (HEAD_SIZE, HEAD_SIZE))
    dma = pltpu.SemaphoreType.DMA
    bf16, f32 = jnp.bfloat16, jnp.float32
    return pl.pallas_call(
        functools.partial(kernel, shape),
        out_shape=pltpu.VMEM(queries.shape, bf16),
        in_specs=[pl.BlockSpec(memory_space=pl.ANY)] * 6,
        scratch_shapes=[
            pltpu.VMEM((shard, 2 * WIDTH), bf16),
            pltpu.VMEM((shard, WIDTH), bf16),
            pltpu.VMEM((shard, 2 * HEAD_SIZE), bf16),
            pltpu.VMEM((shard, 2 * HEAD_SIZE), bf16),
            pltpu.VMEM((2, shard, HEAD_SIZE), bf16),
            pltpu.VMEM((2, HEAD_SIZE, shard), bf16),
            pltpu.VMEM((BLOCKS * pairs * 2, shard, HEAD_SIZE), bf16),
            pltpu.VMEM((BLOCKS * pairs * 2, HEAD_SIZE, shard), bf16),
            pltpu.VMEM((3, CLUSTER, HEAD_SIZE, rows), bf16),
            pltpu.VMEM((span, rows), f32),
            pltpu.VMEM((span, rows), f32),
            pltpu.VMEM((span, rows), bf16),
            pltpu.VMEM((span, rows), bf16),
            pltpu.VMEM((shard, HEAD_SIZE), f32),
            pltpu.VMEM((2, HEAD_SIZE, rows), f32),
            pltpu.VMEM((HEAD_SIZE, HEAD_SIZE), f32),
            pltpu.VMEM((CLUSTER, 8, rows), f32),
            pltpu.VMEM((CLUSTER, 8, rows), f32),
            pltpu.VMEM((2, 8, rows), f32),
            pltpu.VMEM((2, 8, rows), f32),
            pltpu.VMEM((CLUSTER, HEAD_SIZE, rows), f32),
            pltpu.VMEM((CLUSTER, rows, HEAD_SIZE), bf16),
            dma((6,)),
            dma(()),
            dma((2,)),
            dma((2, 2)),
            dma((2, BLOCKS)),
            dma((2, BLOCKS)),
            dma((BLOCKS,)),
            dma((2,)),
        ],
        compiler_params=pltpu.CompilerParams(
            collective_id=0, has_side_effects=True, vmem_limit_bytes=60 * 1024 * 1024
        ),
    )(
        queries, keys, values,
        jnp.asarray(table[:length]), jnp.asarray(np.ascontiguousarray(table.T)), jnp.asarray(far),
    )


def solution(mesh):
    placed = P(("stretch", "seq"), None)
    return jax.shard_map(
        on_device, mesh=mesh, in_specs=(placed,) * 3, out_specs=placed, check_vma=False
    )
```

time: 34.5 us -> 29.7 us (0.86)
  Pallas kernels: 31.2 us -> 27.4 us
  local copies, waits for them, and re-layouts: 3.18 us -> 2.14 us
    pallas_call x1, Pallas kernels: 31.2 us -> 27.4 us  [on_device(): pl.pallas_call(functools.partial(kernel, shape), out_shape=pltpu.VMEM(que...]
    unnamed x1, local copies, waits for them, and re-layouts: 1.82 us -> 0.77 us
where the time goes in v3:
time: 29.7 us; the launch traced here: 29.5 us
  Pallas kernels  27.4 us (92%)
  local copies, waits for them, and re-layouts  2.14 us (7%)
    pallas_call x1, Pallas kernels, on_device(): pl.pallas_call(functools.partial(kernel, shape), out_shape=pltpu.VMEM(que...  27.4 us
    another operation x1, local copies, waits for them, and re-layouts  1.37 us
    unnamed x1, local copies, waits for them, and re-layouts  0.77 us

profile of v3, /device:TPU:25, one launch (start us, length us, event | category | flops | bytes accessed | tf_op | source)
XLA Modules:
  0.0 29.5 jit_solution(17856924461793146759)
XLA Ops:
  0.0 1.4 %jit_solution_.3.far_in = f32[128,128]{1,0:T(8,128)} broadcast(f32[128]{0:T(128)} %constant.8.clone), dimensions={0} | broadcast | bytes 66048 | tf_op jit(solution)
  1.4 27.4 %shard_map.64 = bf16[128,1792]{1,0:T(8,128)(2,1)S(1)} custom-call(bf16[128,1792]{1,0:T(8,128)(2,1)} %q_in.1, bf16[128,256]{1,0:T(8,128)(2,1)} %k_in.1, bf16[128,256]{1,0:T(8,128)(2,1)} %v_in.1, f32[1024,128]{1,0:T(8,128)} %constant.6.clone.rows_in, f32[128,2048]{1,0:T(8,128)} %constant.7.clone.columns_in, f32[128,128]{1,0:T(8,128)} %jit_solution_.3.far_in), custom_call_target="tpu_custom_call" | custom-call | tf_op jit(solution)/shard_map/pallas_call | solution.py:405
  28.8 0.8 %copy.8 = bf16[128,1792]{1,0:T(8,128)(2,1)} copy(bf16[128,1792]{1,0:T(8,128)(2,1)S(1)} %shard_map.64) | data formatting | bytes 917504

commit v4 on v3

--- a/solution.py
+++ b/solution.py
@@ -195,7 +195,7 @@
                 message(t, d, p, block_at(1, h), d + 1, 0, column_sem.at[t, d + 1])
 
     def relayed(d):
-        return (d == 0) | (n < last) | (d == last)
+        return (d == 0) | (d == n - 1)
 
     def pass_on(t, d):
         sources, targets = ((b_peers, a_peers), (a_peers, b_peers))[t]
@@ -306,7 +306,7 @@
     def cross(d):
         await_slots(across_a + 2 * across, cross_sem.at[d])
 
-        @pl.when((n == last - 1) & (d < 2))
+        @pl.when(((n < last) & (d == n)) | ((n == last - 1) & (d == 0)))
         def _():
             pass_up(d)
 
@@ -328,13 +328,13 @@
             pass_on(0, d)
             pass_on(1, d)
 
+        @pl.when((j == 1) & many)
+        def _():
+            column(1, 2)
+
         @pl.when(other)
         def _():
             cross(d)
-
-        @pl.when((j == 1) & many)
-        def _():
-            column(1, 2)
 
         def inner(i, inside):
             line = (a + i) % side_a
@@ -370,7 +370,7 @@
         direct = 2 * (across_a + across_b)
         counts = (
             direct + 1 + lifted + k * (direct + lifted),
-            2 * across * (k + 1 if k < last else 2) + (4 * across if k == last - 1 else 0),
+            2 * across * ((2 if k > 1 else 1) + (k < last) + (k == last - 1)),
         )
 
         @pl.when(n == k)

time: 29.7 us -> 29.2 us (0.983)
  Pallas kernels: 27.4 us -> 26.9 us
    pallas_call x1, Pallas kernels: 27.4 us -> 26.9 us  [on_device(): pl.pallas_call(functools.partial(kernel, shape), out_shape=pltpu.VMEM(que...]
where the time goes in v4:
time: 29.2 us; the launch traced here: 29.1 us
  Pallas kernels  26.9 us (92%)
  local copies, waits for them, and re-layouts  2.14 us (7%)
    pallas_call x1, Pallas kernels, on_device(): pl.pallas_call(functools.partial(kernel, shape), out_shape=pltpu.VMEM(que...  26.9 us
    another operation x1, local copies, waits for them, and re-layouts  1.37 us
    unnamed x1, local copies, waits for them, and re-layouts  0.77 us

profile of v4, /device:TPU:25, one launch (start us, length us, event | category | flops | bytes accessed | tf_op | source)
XLA Modules:
  0.0 29.1 jit_solution(10090928228596116646)
XLA Ops:
  0.0 1.4 %jit_solution_.3.far_in = f32[128,128]{1,0:T(8,128)} broadcast(f32[128]{0:T(128)} %constant.8.clone), dimensions={0} | broadcast | bytes 66048 | tf_op jit(solution)
  1.4 26.9 %shard_map.64 = bf16[128,1792]{1,0:T(8,128)(2,1)S(1)} custom-call(bf16[128,1792]{1,0:T(8,128)(2,1)} %q_in.1, bf16[128,256]{1,0:T(8,128)(2,1)} %k_in.1, bf16[128,256]{1,0:T(8,128)(2,1)} %v_in.1, f32[1024,128]{1,0:T(8,128)} %constant.6.clone.rows_in, f32[128,2048]{1,0:T(8,128)} %constant.7.clone.columns_in, f32[128,128]{1,0:T(8,128)} %jit_solution_.3.far_in), custom_call_target="tpu_custom_call" | custom-call | tf_op jit(solution)/shard_map/pallas_call | solution.py:405
  28.3 0.8 %copy.8 = bf16[128,1792]{1,0:T(8,128)(2,1)} copy(bf16[128,1792]{1,0:T(8,128)(2,1)S(1)} %shard_map.64) | data formatting | bytes 917504

commit v5 on v4

--- a/solution.py
+++ b/solution.py
@@ -74,6 +74,11 @@
 
     a_peers = [pair_at((a + i) % side_a, b) for i in range(1, side_a)]
     b_peers = [pair_at(a, (b + j) % side_b) for j in range(1, side_b)]
+    diagonal = [
+        pair_at((a + i) % side_a, (b + j) % side_b)
+        for i in range(1, side_a)
+        for j in range(1, side_b)
+    ]
     across_a, across_b = len(a_peers), len(b_peers)
     across = across_a * across_b
 
@@ -136,8 +141,6 @@
 
     k_buf[place(0, p, h)] = k_send[h]
     v_buf[place(0, p, h)] = v_send[h]
-    local[3].wait()
-
     pl.semaphore_wait(barrier, 1 + 2 * (across_a + across_b) + 4)
 
     def send(src, dst, sent, received, device):
@@ -162,10 +165,7 @@
         send(src, dst, sent_sem.at[t, group], received, device).start()
 
     def peers(t, d):
-        to_a = cross_sem.at[d] if t == 0 else near_sem.at[1, d]
-        return [(peer, near_sem.at[t, d]) for peer in b_peers] + [
-            (peer, to_a) for peer in a_peers
-        ]
+        return [(peer, near_sem.at[t, d]) for peer in b_peers + a_peers]
 
     query_swap = send(
         q_own.at[:, at((1 - h) * WIDTH, WIDTH, HEAD_SIZE)], q_swap,
@@ -182,6 +182,7 @@
                 first(t, core, block_at(1, core), 1, column_sem.at[t, 1])
 
         first(t, 1 - h, partner, 0, swap_recv.at[0])
+    local[3].wait()
     query_swap.start()
 
     def column(t, d):
@@ -199,31 +200,39 @@
 
     def pass_on(t, d):
         sources, targets = ((b_peers, a_peers), (a_peers, b_peers))[t]
-        await_slots(across_b + t * across_a, near_sem.at[t, d])
+        await_slots(across_a + across_b, near_sem.at[t, d])
 
         @pl.when(relayed(d))
         def _():
             for source in sources:
                 for target in targets:
-                    message(t, d, source, device_at(target, h), d, 1, cross_sem.at[d])
-
-    def pass_up(d):
+                    message(t, d, source, device_at(target, h), d, 1, cross_sem.at[t, d])
+
+    def cross(d):
         for t in range(2):
-            for i in range(1, side_a):
-                for k in range(1, side_b):
-                    pair = pair_at((a + i) % side_a, (b + k) % side_b)
-                    message(t, d, pair, block_at(1, h), d + 1, 1, cross_sem.at[d + 1])
+            await_slots(across, cross_sem.at[t, d])
+
+            @pl.when(((n < last) & (n == d)) | ((n == last - 1) & (d == 0)))
+            def _():
+                for pair in diagonal:
+                    message(t, d, pair, block_at(1, h), d + 1, 1, cross_sem.at[t, d + 1])
 
     def rotate_queries(source, half):
         near, later, far = near_tables[0, :, half], near_tables[1, :, half], far_table[:, :1]
         for c in range(CLUSTER):
             x = source(c).T.astype(jnp.float32)
-            q_rot[0, c, :, half] = turned_columns(x, near)
-            q_rot[1, c, :, half] = turned_columns(x, later)
-            q_rot[2, c, :, half] = turned_columns(x, far)
-
-    def scores(c, d, line, version, causal, into, side):
-        keys = k_buf[pl.ds(place(d, line * side_b, 0), 2 * side_b)].reshape(span, HEAD_SIZE)
+            for version, table in enumerate((near, later, far)):
+                scaled = turned_columns(x, table).astype(jnp.float32) * SCALE
+                high = scaled.astype(jnp.bfloat16)
+                q_rot[version, c, :HEAD_SIZE, half] = high
+                rest = scaled - high.astype(jnp.float32)
+                q_rot[version, c, HEAD_SIZE:, half] = rest.astype(jnp.bfloat16)
+
+    def scores(c, starts, version, causal, into, side):
+        keys = jnp.concatenate(
+            [k_buf[pl.ds(start, 2)].reshape(rows, HEAD_SIZE) for start in starts], axis=0
+        )
+        keys = jnp.concatenate([keys, keys], axis=1)
         found = jnp.dot(keys, q_rot[version, c], preferred_element_type=jnp.float32)
         if causal:
             key = lax.broadcasted_iota(jnp.int32, found.shape, 0)
@@ -233,7 +242,7 @@
         top[side] = jnp.max(found.reshape(span // 8, 8, rows), axis=0)
 
     def weigh(c, causal, source, into, side):
-        new = jnp.max(top[side], axis=0, keepdims=True) * SCALE
+        new = jnp.max(top[side], axis=0, keepdims=True)
         if causal:
             new = jnp.broadcast_to(new, (8, rows))
         else:
@@ -244,15 +253,15 @@
         new = new[:1]
         added = None
         for start in range(0, span, 64):
-            weights = jnp.exp2(source[start : start + 64, :] * SCALE - new)
+            weights = jnp.exp2(source[start : start + 64, :] - new)
             some = jnp.sum(weights.reshape(8, 8, rows), axis=0)
             added = some if added is None else added + some
             into[start : start + 64, :] = weights.astype(jnp.bfloat16)
         total[c] = added if causal else total[c] * fade[side] + added
 
-    def gather(c, d, line, causal, source, side):
+    def gather(c, starts, causal, source, side):
         values = jnp.concatenate(
-            [v_buf[place(d, line * side_b, i)] for i in range(2 * side_b)], axis=1
+            [v_buf[start + i] for start in starts for i in range(2)], axis=1
         )
         product = jnp.dot(values, source[...], preferred_element_type=jnp.float32)
         acc[c] = product if causal else acc[c] * fade[side][:1] + product
@@ -268,15 +277,17 @@
         o_buf[c] = (acc[c] * share).astype(jnp.bfloat16).T
         out[:, at((h * CLUSTER + c) * HEAD_SIZE, HEAD_SIZE, HEAD_SIZE)] = o_buf[c, mine, :]
 
-    def attend(d, line, causal, final):
-        version = jnp.minimum(d, 2)
+    def in_line(d, line):
+        return [place(d, line * side_b + i, 0) for i in range(side_b)]
+
+    def attend(starts, version, causal, final):
         s_buf, w_buf = (s_even, s_odd), (w_even, w_odd)
-        scores(0, d, line, version, causal, s_buf[0], 0)
+        scores(0, starts, version, causal, s_buf[0], 0)
         for c in range(CLUSTER + 1):
             if c + 1 < CLUSTER:
-                scores(c + 1, d, line, version, causal, s_buf[(c + 1) % 2], (c + 1) % 2)
+                scores(c + 1, starts, version, causal, s_buf[(c + 1) % 2], (c + 1) % 2)
             if c > 0:
-                gather(c - 1, d, line, causal, w_buf[(c - 1) % 2], (c - 1) % 2)
+                gather(c - 1, starts, causal, w_buf[(c - 1) % 2], (c - 1) % 2)
                 if final:
                     finish(c - 1)
                     if c > 1:
@@ -301,60 +312,84 @@
         def _():
             column(t, 1)
 
-    attend(0, a, True, False)
-
-    def cross(d):
-        await_slots(across_a + 2 * across, cross_sem.at[d])
-
-        @pl.when(((n < last) & (d == n)) | ((n == last - 1) & (d == 0)))
-        def _():
-            pass_up(d)
+    attend(in_line(0, a), 0, True, False)
+
+    many = n >= 2
+    most = n == last
+    square = side_a == 2 and side_b == 2
+
+    def choose(j, *pairs):
+        found = pairs[-1]
+        for when, value in reversed(pairs[:-1]):
+            found = jnp.where((j == when), value, found)
+        return found
 
     def visit(j, carry):
-        many = n >= 2
-        most = n == last
         d = jnp.where(j < 2, 0, jnp.where((j == 2) | (j == 4), 1, 2))
         d = jnp.where((j == 3) & (n == 1), 1, d)
         d = jnp.where(((j == 5) & most) | (j == 7), last, d)
         other = (j == 1) | (j == 4) | (j > 5) | ((j == 3) & (n == 1)) | ((j == 5) & (n == 2))
-
-        for t, d_in, stage, when in ((0, 2, 1, many), (0, last, 2, most), (1, last, 3, most)):
+        near = jnp.logical_not(other)
+        if square:
+            d = jnp.where(most, choose(j, (1, 0), (4, 2), (6, 3), (3, 2), (7, 2), 1), d)
+            other = jnp.where(most, ((j == 1) | (j == 5)).astype(jnp.int32), other.astype(jnp.int32)) == 1
+            near = (most & (j % 2 == 0)) | (jnp.logical_not(most) & near)
+
+        for t, d_in, stage, when in (
+            (0, 2, 1, many), (1, 2, 1, many), (0, last, 2, most), (1, last, 3, most)
+        ):
             @pl.when((j == stage) & when)
             def _():
                 column(t, d_in)
 
-        @pl.when(jnp.logical_not(other))
+        @pl.when(near)
         def _():
             pass_on(0, d)
             pass_on(1, d)
 
-        @pl.when((j == 1) & many)
-        def _():
-            column(1, 2)
-
-        @pl.when(other)
-        def _():
-            cross(d)
+        late = ((1, 5), (2, 7), (last, 7)) if square else ((1, 4), (2, 6), (last, 7))
+        for d_in, stage, when in [(0, 1, n >= 0), (1, 2, n == 1), (2, 3, n == 2), (1, 4, n == 2)] + [
+            (d_in, stage, most) for d_in, stage in late
+        ]:
+            @pl.when((j == stage) & when)
+            def _():
+                cross(d_in)
 
         def inner(i, inside):
             line = (a + i) % side_a
+            starts = in_line(d, line)
+            if square:
+                pick = [
+                    [place(2, p, 0), place(last, p, 0)],
+                    [place(2, b_peers[0], 0), place(2, a_peers[0], 0)],
+                    [place(last, b_peers[0], 0), place(last, a_peers[0], 0)],
+                ]
+                starts = [
+                    jnp.where(most, choose(j, *zip((3, 4, 6), options), start), start)
+                    for start, *options in zip(starts, *pick)
+                ]
 
             @pl.when((d > 0) | (line < a))
             def _():
-                attend(d, line, False, False)
+                attend(starts, jnp.minimum(d, 2), False, False)
 
             return inside
 
-        ends = jnp.where(other, side_a - jnp.where(j == 2 * n + 1, 1, 0), 1)
-        return lax.fori_loop(jnp.where(other, 1, 0), ends, inner, carry)
+        ends = jnp.where(other, side_a, 1) - jnp.where(j == 2 * n + 1, 1, 0)
+        begins = jnp.where(other, 1, 0)
+        return lax.fori_loop(begins, ends, inner, carry)
 
     lax.fori_loop(1, 2 * (n + 1), visit, 0)
     line = (a + side_a - 1) % side_a
     reached = (n > 0) | (line < a)
+    starts = in_line(n, line)
+    if square:
+        options = [place(2, diagonal[0], 0), place(last, diagonal[0], 0)]
+        starts = [jnp.where(most, option, start) for option, start in zip(options, starts)]
 
     @pl.when(reached)
     def _():
-        attend(n, line, False, True)
+        attend(starts, jnp.minimum(n, 2), False, True)
 
     @pl.when(jnp.logical_not(reached))
     def _():
@@ -415,7 +450,7 @@
             pltpu.VMEM((2, HEAD_SIZE, shard), bf16),
             pltpu.VMEM((BLOCKS * pairs * 2, shard, HEAD_SIZE), bf16),
             pltpu.VMEM((BLOCKS * pairs * 2, HEAD_SIZE, shard), bf16),
-            pltpu.VMEM((3, CLUSTER, HEAD_SIZE, rows), bf16),
+            pltpu.VMEM((3, CLUSTER, 2 * HEAD_SIZE, rows), bf16),
             pltpu.VMEM((span, rows), f32),
             pltpu.VMEM((span, rows), f32),
             pltpu.VMEM((span, rows), bf16),
@@ -435,7 +470,7 @@
             dma((2, 2)),
             dma((2, BLOCKS)),
             dma((2, BLOCKS)),
-            dma((BLOCKS,)),
+            dma((2, BLOCKS)),
             dma((2,)),
         ],
         compiler_params=pltpu.CompilerParams(

time: 29.2 us -> 27.5 us (0.942)
  Pallas kernels: 26.9 us -> 25.2 us
    pallas_call x1, Pallas kernels: 26.9 us -> 25.2 us  [on_device(): pl.pallas_call(functools.partial(kernel, shape), out_shape=pltpu.VMEM(que...]
where the time goes in v5:
time: 27.5 us; the launch traced here: 27.3 us
  Pallas kernels  25.2 us (92%)
  local copies, waits for them, and re-layouts  2.14 us (8%)
    pallas_call x1, Pallas kernels, on_device(): pl.pallas_call(functools.partial(kernel, shape), out_shape=pltpu.VMEM(que...  25.2 us
    another operation x1, local copies, waits for them, and re-layouts  1.37 us
    unnamed x1, local copies, waits for them, and re-layouts  0.77 us

profile of v5, /device:TPU:25, one launch (start us, length us, event | category | flops | bytes accessed | tf_op | source)
XLA Modules:
  0.0 27.3 jit_solution(11807258618293889585)
XLA Ops:
  0.0 1.4 %jit_solution_.3.far_in = f32[128,128]{1,0:T(8,128)} broadcast(f32[128]{0:T(128)} %constant.8.clone), dimensions={0} | broadcast | bytes 66048 | tf_op jit(solution)
  1.4 25.2 %shard_map.64 = bf16[128,1792]{1,0:T(8,128)(2,1)S(1)} custom-call(bf16[128,1792]{1,0:T(8,128)(2,1)} %q_in.1, bf16[128,256]{1,0:T(8,128)(2,1)} %k_in.1, bf16[128,256]{1,0:T(8,128)(2,1)} %v_in.1, f32[1024,128]{1,0:T(8,128)} %constant.6.clone.rows_in, f32[128,2048]{1,0:T(8,128)} %constant.7.clone.columns_in, f32[128,128]{1,0:T(8,128)} %jit_solution_.3.far_in), custom_call_target="tpu_custom_call" | custom-call | tf_op jit(solution)/shard_map/pallas_call | solution.py:440
  26.6 0.8 %copy.8 = bf16[128,1792]{1,0:T(8,128)(2,1)} copy(bf16[128,1792]{1,0:T(8,128)(2,1)S(1)} %shard_map.64) | data formatting | bytes 917504

commit v6 on v5

--- a/solution.py
+++ b/solution.py
@@ -229,17 +229,19 @@
                 q_rot[version, c, HEAD_SIZE:, half] = rest.astype(jnp.bfloat16)
 
     def scores(c, starts, version, causal, into, side):
-        keys = jnp.concatenate(
-            [k_buf[pl.ds(start, 2)].reshape(rows, HEAD_SIZE) for start in starts], axis=0
-        )
-        keys = jnp.concatenate([keys, keys], axis=1)
-        found = jnp.dot(keys, q_rot[version, c], preferred_element_type=jnp.float32)
-        if causal:
-            key = lax.broadcasted_iota(jnp.int32, found.shape, 0)
-            row = b * rows + lax.broadcasted_iota(jnp.int32, found.shape, 1)
-            found = jnp.where(row >= key, found, MASKED)
-        into[...] = found
-        top[side] = jnp.max(found.reshape(span // 8, 8, rows), axis=0)
+        highest = None
+        for i in range(2 * len(starts)):
+            keys = k_buf[starts[i // 2] + i % 2]
+            keys = jnp.concatenate([keys, keys], axis=1)
+            found = jnp.dot(keys, q_rot[version, c], preferred_element_type=jnp.float32)
+            if causal:
+                key = i * shard + lax.broadcasted_iota(jnp.int32, found.shape, 0)
+                row = b * rows + lax.broadcasted_iota(jnp.int32, found.shape, 1)
+                found = jnp.where(row >= key, found, MASKED)
+            into[i * shard : (i + 1) * shard, :] = found
+            some = jnp.max(found.reshape(shard // 8, 8, rows), axis=0)
+            highest = some if highest is None else jnp.maximum(highest, some)
+        top[side] = highest
 
     def weigh(c, causal, source, into, side):
         new = jnp.max(top[side], axis=0, keepdims=True)
@@ -260,10 +262,13 @@
         total[c] = added if causal else total[c] * fade[side] + added
 
     def gather(c, starts, causal, source, side):
-        values = jnp.concatenate(
-            [v_buf[start + i] for start in starts for i in range(2)], axis=1
-        )
-        product = jnp.dot(values, source[...], preferred_element_type=jnp.float32)
+        product = None
+        for i, start in enumerate(starts):
+            values = jnp.concatenate([v_buf[start], v_buf[start + 1]], axis=1)
+            some = jnp.dot(
+                values, source[i * rows : (i + 1) * rows, :], preferred_element_type=jnp.float32
+            )
+            product = some if product is None else product + some
         acc[c] = product if causal else acc[c] * fade[side][:1] + product
 
     def result(c):

time: 27.5 us -> 26.9 us (0.978)
  Pallas kernels: 25.2 us -> 24.6 us
    pallas_call x1, Pallas kernels: 25.2 us -> 24.6 us  [on_device(): pl.pallas_call(functools.partial(kernel, shape), out_shape=pltpu.VMEM(que...]
where the time goes in v6:
time: 26.9 us; the launch traced here: 26.7 us
  Pallas kernels  24.6 us (91%)
  local copies, waits for them, and re-layouts  2.14 us (8%)
    pallas_call x1, Pallas kernels, on_device(): pl.pallas_call(functools.partial(kernel, shape), out_shape=pltpu.VMEM(que...  24.6 us
    another operation x1, local copies, waits for them, and re-layouts  1.37 us
    unnamed x1, local copies, waits for them, and re-layouts  0.77 us

profile of v6, /device:TPU:25, one launch (start us, length us, event | category | flops | bytes accessed | tf_op | source)
XLA Modules:
  0.0 26.7 jit_solution(8974319853481960620)
XLA Ops:
  0.0 1.4 %jit_solution_.3.far_in = f32[128,128]{1,0:T(8,128)} broadcast(f32[128]{0:T(128)} %constant.8.clone), dimensions={0} | broadcast | bytes 66048 | tf_op jit(solution)
  1.4 24.6 %shard_map.64 = bf16[128,1792]{1,0:T(8,128)(2,1)S(1)} custom-call(bf16[128,1792]{1,0:T(8,128)(2,1)} %q_in.1, bf16[128,256]{1,0:T(8,128)(2,1)} %k_in.1, bf16[128,256]{1,0:T(8,128)(2,1)} %v_in.1, f32[1024,128]{1,0:T(8,128)} %constant.6.clone.rows_in, f32[128,2048]{1,0:T(8,128)} %constant.7.clone.columns_in, f32[128,128]{1,0:T(8,128)} %jit_solution_.3.far_in), custom_call_target="tpu_custom_call" | custom-call | tf_op jit(solution)/shard_map/pallas_call | solution.py:445
  26.0 0.8 %copy.8 = bf16[128,1792]{1,0:T(8,128)(2,1)} copy(bf16[128,1792]{1,0:T(8,128)(2,1)S(1)} %shard_map.64) | data formatting | bytes 917504

commit v7 on v6

--- a/solution.py
+++ b/solution.py
@@ -93,12 +93,12 @@
 
     local = [
         (k_in, k_own, 0),
-        (rows_in.at[at(p * rows + h * shard, shard, shard), :], row_table, 1),
-        (v_in, v_own, 2),
-        (q_in, q_own, 3),
-        (columns_in.at[:, at(p * rows, rows, rows)], near_tables.at[0], 4),
-        (columns_in.at[:, at(length + p * rows, rows, rows)], near_tables.at[1], 4),
-        (far_in, far_table, 5),
+        (rows_in.at[at(p * rows + h * shard, shard, shard), :], row_table, 0),
+        (v_in, v_own, 0),
+        (q_in, q_own, 1),
+        (columns_in.at[:, at(p * rows, rows, rows)], near_tables.at[0], 2),
+        (columns_in.at[:, at(length + p * rows, rows, rows)], near_tables.at[1], 2),
+        (far_in, far_table, 3),
     ]
     local = [pltpu.make_async_copy(src, dst, local_sem.at[i]) for src, dst, i in local]
     for copy in local:
@@ -126,8 +126,8 @@
             greet(device_at(peer, core))
     greet(partner)
 
-    for copy in local[:3]:
-        copy.wait()
+    early = q_own.at[:, pl.ds(0, 6 * HEAD_SIZE)]
+    pltpu.make_async_copy(early, early, local_sem.at[0]).wait()
     for head in range(KEY_VALUE_HEADS):
         columns = slice(head * HEAD_SIZE, (head + 1) * HEAD_SIZE)
         k_send[head] = turned_rows(k_own[:, columns], row_table[...])
@@ -165,7 +165,7 @@
         send(src, dst, sent_sem.at[t, group], received, device).start()
 
     def peers(t, d):
-        return [(peer, near_sem.at[t, d]) for peer in b_peers + a_peers]
+        return [(peer, near_sem.at[t if isinstance(d, int) and d == 0 else d + 1]) for peer in b_peers + a_peers]
 
     query_swap = send(
         q_own.at[:, at((1 - h) * WIDTH, WIDTH, HEAD_SIZE)], q_swap,
@@ -179,34 +179,35 @@
         @pl.when(n < last)
         def _():
             for core in range(2):
-                first(t, core, block_at(1, core), 1, column_sem.at[t, 1])
+                first(t, core, block_at(1, core), 1, column_sem.at[t, 0])
 
         first(t, 1 - h, partner, 0, swap_recv.at[0])
     local[3].wait()
     query_swap.start()
 
     def column(t, d):
-        await_slots(1, column_sem.at[t, d])
+        await_slots(1, column_sem.at[t, d - 1])
         for peer, received in peers(t, d):
             message(t, d, p, device_at(peer, h), d, 0, received)
 
         if not (isinstance(d, int) and d == last):
             @pl.when(n < last)
             def _():
-                message(t, d, p, block_at(1, h), d + 1, 0, column_sem.at[t, d + 1])
+                message(t, d, p, block_at(1, h), d + 1, 0, column_sem.at[t, d])
 
     def relayed(d):
         return (d == 0) | (d == n - 1)
 
-    def pass_on(t, d):
-        sources, targets = ((b_peers, a_peers), (a_peers, b_peers))[t]
-        await_slots(across_a + across_b, near_sem.at[t, d])
+    def pass_on(sides, d, received):
+        await_slots(len(sides) * (across_a + across_b), received)
 
         @pl.when(relayed(d))
         def _():
-            for source in sources:
-                for target in targets:
-                    message(t, d, source, device_at(target, h), d, 1, cross_sem.at[t, d])
+            for t in sides:
+                sources, targets = ((b_peers, a_peers), (a_peers, b_peers))[t]
+                for source in sources:
+                    for target in targets:
+                        message(t, d, source, device_at(target, h), d, 1, cross_sem.at[t, d])
 
     def cross(d):
         for t in range(2):
@@ -304,14 +305,14 @@
 
     for copy in local[6:]:
         copy.wait()
-    pltpu.make_async_copy(near_tables, near_tables, local_sem.at[4]).wait()
+    pltpu.make_async_copy(near_tables, near_tables, local_sem.at[2]).wait()
     rotate_queries(lambda c: q_own[:, at(h * WIDTH + c * HEAD_SIZE, HEAD_SIZE, HEAD_SIZE)], mine)
     query_swap.wait_recv()
     rotate_queries(lambda c: q_swap[:, c * HEAD_SIZE : (c + 1) * HEAD_SIZE], theirs)
     await_slots(1, swap_recv.at[0])
 
     for t in range(2):
-        pass_on(t, 0)
+        pass_on((t,), 0, near_sem.at[t])
 
         @pl.when(n > 0)
         def _():
@@ -347,11 +348,6 @@
             def _():
                 column(t, d_in)
 
-        @pl.when(near)
-        def _():
-            pass_on(0, d)
-            pass_on(1, d)
-
         late = ((1, 5), (2, 7), (last, 7)) if square else ((1, 4), (2, 6), (last, 7))
         for d_in, stage, when in [(0, 1, n >= 0), (1, 2, n == 1), (2, 3, n == 2), (1, 4, n == 2)] + [
             (d_in, stage, most) for d_in, stage in late
@@ -359,6 +355,10 @@
             @pl.when((j == stage) & when)
             def _():
                 cross(d_in)
+
+        @pl.when(near)
+        def _():
+            pass_on((0, 1), d, near_sem.at[d + 1])
 
         def inner(i, inside):
             line = (a + i) % side_a
@@ -469,12 +469,12 @@
             pltpu.VMEM((2, 8, rows), f32),
             pltpu.VMEM((CLUSTER, HEAD_SIZE, rows), f32),
             pltpu.VMEM((CLUSTER, rows, HEAD_SIZE), bf16),
-            dma((6,)),
+            dma((4,)),
             dma(()),
             dma((2,)),
             dma((2, 2)),
-            dma((2, BLOCKS)),
-            dma((2, BLOCKS)),
+            dma((2, BLOCKS - 1)),
+            dma((BLOCKS + 1,)),
             dma((2, BLOCKS)),
             dma((2,)),
         ],

time: 26.9 us -> 26.8 us (level)
  no operation moved by 1% of the time
where the time goes in v7:
time: 26.8 us; the launch traced here: 26.7 us
  Pallas kernels  24.5 us (91%)
  local copies, waits for them, and re-layouts  2.14 us (8%)
    pallas_call x1, Pallas kernels, on_device(): pl.pallas_call(functools.partial(kernel, shape), out_shape=pltpu.VMEM(que...  24.5 us
    another operation x1, local copies, waits for them, and re-layouts  1.37 us
    unnamed x1, local copies, waits for them, and re-layouts  0.77 us

profile of v7, /device:TPU:25, one launch (start us, length us, event | category | flops | bytes accessed | tf_op | source)
XLA Modules:
  0.0 26.7 jit_solution(5444538406896524372)
XLA Ops:
  0.0 1.4 %jit_solution_.3.far_in = f32[128,128]{1,0:T(8,128)} broadcast(f32[128]{0:T(128)} %constant.8.clone), dimensions={0} | broadcast | bytes 66048 | tf_op jit(solution)
  1.4 24.5 %shard_map.64 = bf16[128,1792]{1,0:T(8,128)(2,1)S(1)} custom-call(bf16[128,1792]{1,0:T(8,128)(2,1)} %q_in.1, bf16[128,256]{1,0:T(8,128)(2,1)} %k_in.1, bf16[128,256]{1,0:T(8,128)(2,1)} %v_in.1, f32[1024,128]{1,0:T(8,128)} %constant.6.clone.rows_in, f32[128,2048]{1,0:T(8,128)} %constant.7.clone.columns_in, f32[128,128]{1,0:T(8,128)} %jit_solution_.3.far_in), custom_call_target="tpu_custom_call" | custom-call | tf_op jit(solution)/shard_map/pallas_call | solution.py:445
  25.9 0.8 %copy.8 = bf16[128,1792]{1,0:T(8,128)(2,1)} copy(bf16[128,1792]{1,0:T(8,128)(2,1)S(1)} %shard_map.64) | data formatting | bytes 917504

commit v8 on v7

--- a/solution.py
+++ b/solution.py
@@ -270,7 +270,11 @@
                 values, source[i * rows : (i + 1) * rows, :], preferred_element_type=jnp.float32
             )
             product = some if product is None else product + some
-        acc[c] = product if causal else acc[c] * fade[side][:1] + product
+        for i in range(0, HEAD_SIZE, 32):
+            some = product[i : i + 32]
+            acc[c, i : i + 32, :] = (
+                some if causal else acc[c, i : i + 32, :] * fade[side][:1] + some
+            )
 
     def result(c):
         where = at((h * CLUSTER + c) * HEAD_SIZE, HEAD_SIZE, HEAD_SIZE)

time: 26.8 us -> 26.8 us (level)
  no operation moved by 1% of the time
where the time goes in v8:
time: 26.8 us; the launch traced here: 26.7 us
  Pallas kernels  24.5 us (91%)
  local copies, waits for them, and re-layouts  2.14 us (8%)
    pallas_call x1, Pallas kernels, on_device(): pl.pallas_call(functools.partial(kernel, shape), out_shape=pltpu.VMEM(que...  24.5 us
    another operation x1, local copies, waits for them, and re-layouts  1.37 us
    unnamed x1, local copies, waits for them, and re-layouts  0.77 us

profile of v8, /device:TPU:25, one launch (start us, length us, event | category | flops | bytes accessed | tf_op | source)
XLA Modules:
  0.0 26.7 jit_solution(2362637166386650435)
XLA Ops:
  0.0 1.4 %jit_solution_.3.far_in = f32[128,128]{1,0:T(8,128)} broadcast(f32[128]{0:T(128)} %constant.8.clone), dimensions={0} | broadcast | bytes 66048 | tf_op jit(solution)
  1.4 24.5 %shard_map.64 = bf16[128,1792]{1,0:T(8,128)(2,1)S(1)} custom-call(bf16[128,1792]{1,0:T(8,128)(2,1)} %q_in.1, bf16[128,256]{1,0:T(8,128)(2,1)} %k_in.1, bf16[128,256]{1,0:T(8,128)(2,1)} %v_in.1, f32[1024,128]{1,0:T(8,128)} %constant.6.clone.rows_in, f32[128,2048]{1,0:T(8,128)} %constant.7.clone.columns_in, f32[128,128]{1,0:T(8,128)} %jit_solution_.3.far_in), custom_call_target="tpu_custom_call" | custom-call | tf_op jit(solution)/shard_map/pallas_call | solution.py:449
  25.9 0.8 %copy.8 = bf16[128,1792]{1,0:T(8,128)(2,1)} copy(bf16[128,1792]{1,0:T(8,128)(2,1)S(1)} %shard_map.64) | data formatting | bytes 917504
